TPU v7x, 128 devices: a whole 4x4x4 slice. The times are simulated.
128 devices in a mesh: row: 8 (over z, x_lo), col: 16 (over y, x_hi, core).
Axes of the slice: x: 4 (x_hi: 2, x_lo: 2; x = x_hi * 2 + x_lo), y: 4, z: 4, core: 2. Of those that a mesh axis runs over, the one named last changes fastest.
Arguments:
- tokens: bfloat16 [256, 16384], P('row', 'col'), may hold values from -6 to 6
- probe_words: int32 [256, 512], P(None, 'col'), may hold values from -2147483648 to 2147483646, as said below
- token_ids: int32 [256], replicated, may hold values from 0 to 128255
- loss_weight: float32 [128256], replicated, may hold values from 0.5 to 2
- gate_weight: bfloat16 [16384, 26624], P('col', 'row'), may hold values from -0.046875 to 0.046875
- up_weight: bfloat16 [16384, 26624], P('col', 'row'), may hold values from -0.046875 to 0.046875
- down_weight: bfloat16 [26624, 16384], P('row', 'col'), may hold values from -0.0390625 to 0.0390625
Outputs:
- hvp: float32 [256, 16384], P('row', 'col')
Inputs may be any that keep to these rules, and one draw needn't show every extreme that they name: `probe_words`: every bit of every word is an independent fair sign bit; bit k of word j of token t is the probe sign of feature 32 j + k of that token (set: +1, clear: -1).
All inputs are finite; a program needn't handle non-finite values.
Results may differ from a plain program's by a relative error of at most 0.0036.
Values may be sent and summed in bfloat16 or wider, within the bound.
A program may use at most 128 MiB of HBM per device.

v0:
```python
import jax
import jax.numpy as jnp
from jax import lax
from jax.sharding import PartitionSpec as P


def copy_for_each(x, axis):
    copies = jnp.broadcast_to(x, (lax.axis_size(axis), *x.shape))
    return lax.all_to_all(copies, axis, split_axis=0, concat_axis=0, tiled=True)


def laid_out(pieces, dim):
    dims = list(pieces.shape[1:])
    dims[dim] *= pieces.shape[0]
    return jnp.moveaxis(pieces, 0, dim).reshape(dims)


def gathered_copies(x, axis, dim):
    pieces = copy_for_each(x, axis)
    return laid_out(pieces, dim)


def side_by_side(arrays, axis, dim, along):
    both = jnp.concatenate(arrays, axis=along)
    result, at, finished = (lax.all_gather(both, axis, axis=dim, tiled=True), 0, [])
    for a in arrays:
        finished.append(lax.slice_in_dim(result, at, at + a.shape[along], axis=along))
        at += a.shape[along]
    return tuple(finished)


def in_blocks(x, dim, peers):
    before, after = (x.shape[:dim], x.shape[dim + 1 :])
    return jnp.moveaxis(x.reshape(*before, peers, -1, *after), dim, 0)


def summed_on_arrival(x, axis, dim):
    pieces = in_blocks(x, dim, lax.axis_size(axis))
    arrived = lax.all_to_all(pieces, axis, split_axis=0, concat_axis=0, tiled=True)
    return arrived.sum(axis=0)


def unpack_signs(packed):
    shifts = jnp.arange(32, dtype=jnp.int32)
    bit_vals = jnp.bitwise_and(jnp.right_shift(packed[:, :, None], shifts), 1)
    return (2 * bit_vals - 1).reshape(packed.shape[0], -1).astype(jnp.bfloat16)


def silu_parts(pre_act):
    sigmoid_pre = jax.nn.sigmoid(pre_act)
    active = pre_act * sigmoid_pre
    slopes = sigmoid_pre * (1.0 + pre_act * (1.0 - sigmoid_pre))
    curves = sigmoid_pre * (1.0 - sigmoid_pre) * (2.0 + pre_act * (1.0 - 2.0 * sigmoid_pre))
    return (active, slopes, curves)


def matmul(left_rows, weight):
    return jnp.dot(left_rows, weight, preferred_element_type=jnp.float32)


def matmul_trans(left_rows, weight):
    return lax.dot_general(
        left_rows, weight, (((1,), (1,)), ((), ())), preferred_element_type=jnp.float32
    )


def paired(first_rows, second_rows, weight, product):
    return (product(first_rows, weight), product(second_rows, weight))


def project_in(tok_rows, probe_rows, gate_weight, up_weight):
    gate_pre, gate_tan = paired(tok_rows, probe_rows, gate_weight, matmul)
    up_pre, up_tan = paired(tok_rows, probe_rows, up_weight, matmul)
    return (gate_pre, up_pre, gate_tan, up_tan)


def hidden_pair(gate_pre, up_pre, gate_tan, up_tan):
    active, slopes, curves = silu_parts(gate_pre)
    hidden = (active * up_pre).astype(jnp.bfloat16)
    hidden_tan = (slopes * gate_tan * up_pre + active * up_tan).astype(jnp.bfloat16)
    return (hidden, hidden_tan)


def back_pair(gate_pre, up_pre, gate_tan, up_tan, backward, back_tan):
    active, slopes, curves = silu_parts(gate_pre)
    gate_back = (
        back_tan * up_pre * slopes
        + backward * up_tan * slopes
        + backward * up_pre * curves * gate_tan
    ).astype(jnp.bfloat16)
    up_back = (back_tan * active + backward * slopes * gate_tan).astype(jnp.bfloat16)
    return (gate_back, up_back)


def on_device(tokens, probe_words, token_ids, loss_weight, gate_weight, up_weight, down_weight):
    gathered = gathered_copies(tokens, "row", 0)
    all_rows = gathered.shape[0]
    probe = unpack_signs(probe_words)
    hidden_width = gate_weight.shape[1]
    row_rows = all_rows // lax.axis_size("row")
    shares = lax.psum_scatter(
        jnp.concatenate(project_in(gathered, probe, gate_weight, up_weight), axis=1),
        "col",
        scatter_dimension=0,
        tiled=True,
    )
    gate_pre = shares[:, :hidden_width]
    up_pre = shares[:, hidden_width : 2 * hidden_width]
    gate_tan = shares[:, 2 * hidden_width : 3 * hidden_width]
    up_tan = shares[:, 3 * hidden_width :]
    hidden_share, tan_share = hidden_pair(gate_pre, up_pre, gate_tan, up_tan)
    hidden, hidden_tan = side_by_side((hidden_share, tan_share), "col", 0, 1)
    out_pieces = paired(hidden, hidden_tan, down_weight, matmul)
    output, out_tan = lax.psum((out_pieces[0], out_pieces[1]), "row")
    weight_tok = jnp.take(loss_weight, token_ids)[:, None]
    cotangent = (weight_tok * (gathered.astype(jnp.float32) + output)).astype(jnp.bfloat16)
    cot_tan = weight_tok * (probe.astype(jnp.float32) + out_tan)
    cot_half = cot_tan.astype(jnp.bfloat16)
    back_shares = lax.psum_scatter(
        jnp.concatenate(paired(cotangent, cot_half, down_weight, matmul_trans), axis=1),
        "col",
        scatter_dimension=0,
        tiled=True,
    )
    gate_share, up_share = back_pair(
        gate_pre,
        up_pre,
        gate_tan,
        up_tan,
        back_shares[:, :hidden_width],
        back_shares[:, hidden_width:],
    )
    gate_back, up_back = side_by_side((gate_share, up_share), "col", 0, 1)
    summed = summed_on_arrival(
        matmul_trans(gate_back, gate_weight) + matmul_trans(up_back, up_weight), "row", 0
    )
    own_tan = lax.dynamic_slice_in_dim(cot_tan, lax.axis_index("row") * row_rows, row_rows, 0)
    return own_tan + summed


def solution(mesh):
    return jax.shard_map(
        on_device,
        mesh=mesh,
        in_specs=(
            P("row", "col"),
            P(None, "col"),
            P(),
            P(),
            P("col", "row"),
            P("col", "row"),
            P("row", "col"),
        ),
        out_specs=P("row", "col"),
        check_vma=False,
    )
```

profile of v0, /device:TPU:0, one launch (start us, length us, event | category | flops | bytes accessed | tf_op | source)
XLA Modules:
  0.0 535.4 jit_solution(15537788906171822060)
XLA Ops:
  6.5 1.7 broadcast_in_dim.16
  8.3 6.4 %all-to-all-start = ((bf16[8,32,1024]{2,1,0:T(8,128)(2,1)}), bf16[8,32,1024]{2,1,0:T(8,128)(2,1)S(1)}, u32[]{:S(2)}, u32[]{:S(2)}) async-start(bf16[8,32,1024]{2,1,0:T(8,128)(2,1)} %broadcast_in_dim.16), calls=%async_computation | async-start | bytes 1048576 | tf_op jit(solution)/shard_map/all_to_all | solution.py:9
  15.9 6.7 %fusion.25 = f32[256,3328]{1,0:T(8,128)} fusion(bf16[1024,3328]{1,0:T(8,128)(2,1)} %param.11, s32[256,1024]{1,0:T(8,128)S(1)} %copy.9, s32[1024]{0:T(1024)S(1)} %shift_right_arithmetic.23), kind=kOutput, calls=%fused_computation.41 | convolution fusion | flops 1746141184 | bytes 11276288 | tf_op jit(solution)/shard_map/dot_general | solution.py:58
  22.6 6.6 %fusion.26 = f32[256,3328]{1,0:T(8,128)} fusion(bf16[1024,3328]{1,0:T(8,128)(2,1)} %param.12, s32[256,1024]{1,0:T(8,128)S(1)} %copy.9, s32[1024]{0:T(1024)S(1)} %shift_right_arithmetic.23), kind=kOutput, calls=%fused_computation.42 | convolution fusion | flops 1746141184 | bytes 11276288 | tf_op jit(solution)/shard_map/dot_general | solution.py:58
  29.3 5.0 fusion.23
  34.3 2.0 fusion.24
  37.3 5.1 pad_maximum_fusion
  42.5 128.6 %reduce-scatter.3.cloned.1.call-done = f32[16,13312]{1,0:T(8,128)} async-done(((f32[256,13312]{1,0:T(8,128)}), f32[16,13312]{1,0:T(8,128)}) %reduce-scatter.3.cloned.1.call-update) | async-done | bytes 851984 | tf_op jit(solution)/shard_map/reduce_scatter | solution.py:101
  171.1 1.4 multiply_convert_fusion.2
  173.3 50.1 %all-gather.3.cloned.1.call-done = bf16[256,6656]{1,0:T(8,128)(2,1)} async-done(((bf16[16,6656]{1,0:T(8,128)(2,1)}), bf16[256,6656]{1,0:T(8,128)(2,1)}) %all-gather.3.cloned.1.call-update) | async-done | bytes 3407888 | tf_op jit(solution)/shard_map/all_gather | solution.py:25
  223.4 6.5 %fusion.4 = f32[256,1024]{1,0:T(8,128)} fusion(bf16[3328,1024]{1,0:T(8,128)(2,1)} %param.13, bf16[256,6656]{1,0:T(8,128)(2,1)} %all-gather.3.cloned.1.call-done), kind=kOutput, calls=%fused_computation.7 | convolution fusion | flops 1744830464 | bytes 9568256 | tf_op jit(solution)/shard_map/dot_general | solution.py:58
  229.9 6.0 %fusion.6 = f32[256,1024]{1,0:T(8,128)} fusion(bf16[3328,1024]{1,0:T(8,128)(2,1)} %param.13, bf16[256,6656]{1,0:T(8,128)(2,1)S(1)} %copy-done.6), kind=kOutput, calls=%fused_computation.9 | convolution fusion | flops 1744830464 | bytes 9568256 | tf_op jit(solution)/shard_map/dot_general | solution.py:58
  236.2 1.7 gather_fusion
  238.0 101.8 %all-reduce.3.cloned.1.call-done = (f32[256,1024]{1,0:T(8,128)}, f32[256,1024]{1,0:T(8,128)}) async-done(((f32[256,1024]{1,0:T(8,128)}, f32[256,1024]{1,0:T(8,128)}), (f32[256,1024]{1,0:T(8,128)}, f32[256,1024]{1,0:T(8,128)})) %all-reduce.3.cloned.1.call-update) | async-done | bytes 2097168 | tf_op jit(solution)/shard_map/psum | solution.py:114
  339.8 1.6 add_multiply_fusion
  341.5 5.1 fusion.12
  346.6 2.1 fusion.11
  348.7 3.6 pad_maximum_fusion.1
  352.4 91.2 %reduce-scatter.5.cloned.1.call-done = f32[16,6656]{1,0:T(8,128)} async-done(((f32[256,6656]{1,0:T(8,128)}), f32[16,6656]{1,0:T(8,128)}) %reduce-scatter.5.cloned.1.call-update) | async-done | bytes 426000 | tf_op jit(solution)/shard_map/reduce_scatter | solution.py:119
  445.5 50.5 %all-gather.5.cloned.1.call-done = bf16[256,6656]{1,0:T(8,128)(2,1)} async-done(((bf16[16,6656]{1,0:T(8,128)(2,1)}), bf16[256,6656]{1,0:T(8,128)(2,1)}) %all-gather.5.cloned.1.call-update) | async-done | bytes 3407888 | tf_op jit(solution)/shard_map/all_gather | solution.py:25
  496.1 5.5 %fusion = f32[256,1024]{1,0:T(8,128)S(1)} fusion(bf16[1024,3328]{1,0:T(8,128)(2,1)} %param.12, bf16[256,6656]{1,0:T(8,128)(2,1)} %all-gather.5.cloned.1.call-done), kind=kOutput, calls=%fused_computation.3 | convolution fusion | flops 1744830464 | bytes 9568256 | tf_op jit(solution)/shard_map/dot_general | solution.py:62
  501.6 5.9 %fusion.8 = f32[256,1024]{1,0:T(8,128)} fusion(f32[256,1024]{1,0:T(8,128)S(1)} %fusion, bf16[1024,3328]{1,0:T(8,128)(2,1)} %param.11, bf16[256,6656]{1,0:T(8,128)(2,1)S(1)} %copy-done.7), kind=kOutput, calls=%fused_computation.11 | convolution fusion | flops 1745092608 | bytes 10616832 | tf_op jit(solution)/shard_map/dot_general | solution.py:62
  507.5 4.4 all-to-all-start.1
  512.0 16.2 %all-to-all-done.1 = f32[8,32,1024]{2,1,0:T(8,128)S(1)} async-done(((f32[8,32,1024]{2,1,0:T(8,128)}), f32[8,32,1024]{2,1,0:T(8,128)S(1)}, u32[]{:S(2)}, u32[]{:S(2)}) %all-to-all-start.1) | async-done | bytes 1048608 | tf_op jit(solution)/shard_map/all_to_all | solution.py:39
  (49 shorter events, 6.2 us)
Async XLA Ops:
  6.5 229.7 %copy-start = (f32[128256]{0:T(1024)S(1)}, f32[128256]{0:T(1024)}, u32[]{:S(2)}) copy-start(f32[128256]{0:T(1024)} %param.10) | copy-start | bytes 1539076
  8.3 21.0 %all-to-all-start = ((bf16[8,32,1024]{2,1,0:T(8,128)(2,1)}), bf16[8,32,1024]{2,1,0:T(8,128)(2,1)S(1)}, u32[]{:S(2)}, u32[]{:S(2)}) async-start(bf16[8,32,1024]{2,1,0:T(8,128)(2,1)} %broadcast_in_dim.16), calls=%async_computation | async-start | bytes 1048576 | tf_op jit(solution)/shard_map/all_to_all | solution.py:9
  14.6 156.5 %reduce-scatter.3.cloned.1.call-start = ((), (), s32[]{:S(2)}) async-start(), calls=%async_computation.4 | async-start | bytes 14483456 | tf_op jit(solution)/shard_map/reduce_scatter | solution.py:101
  29.3 5.0 slice-start.2
  29.3 5.0 slice-start.3
  34.3 2.0 copy-start.1
  34.3 3.0 copy-start.2
  42.5 180.9 %all-gather.3.cloned.1.call-start = ((), (), s32[]{:S(2)}) async-start(), calls=%async_computation.5 | async-start | bytes 3620864 | tf_op jit(solution)/shard_map/all_gather | solution.py:25
  173.2 166.6 %all-reduce.3.cloned.1.call-start = ((), (), s32[]{:S(2)}) async-start(), calls=%async_computation.8 | async-start | bytes 4194304 | tf_op jit(solution)/shard_map/psum | solution.py:114
  223.4 6.5 %copy-start.6 = (bf16[256,6656]{1,0:T(8,128)(2,1)S(1)}, bf16[256,6656]{1,0:T(8,128)(2,1)}, u32[]{:S(2)}) copy-start(bf16[256,6656]{1,0:T(8,128)(2,1)} %all-gather.3.cloned.1.call-done) | copy-start | bytes 10223620
  229.9 6.3 %copy-start.5 = (s32[256]{0:T(256)S(1)}, s32[256]{0:T(256)}, u32[]{:S(2)}) copy-start(s32[256]{0:T(256)} %param.9) | copy-start | bytes 3076
  235.9 207.6 %reduce-scatter.5.cloned.1.call-start = ((), (), s32[]{:S(2)}) async-start(), calls=%async_computation.6 | async-start | bytes 7241728 | tf_op jit(solution)/shard_map/reduce_scatter | solution.py:119
  339.8 6.8 %slice-start = ((s8[6815744]{0:T(1024)(128)(4,1)}), s8[4194304]{0:T(1024)(128)(4,1)S(1)}, s32[]{:S(2)}) async-start(s8[6815744]{0:T(1024)(128)(4,1)} %bitcast.17), calls=%async_computation.9 | async-start | bytes 8388608
  339.8 6.8 %copy-start.4 = (f32[256,1024]{1,0:T(8,128)S(1)}, f32[256,1024]{1,0:T(8,128)}, u32[]{:S(2)}) copy-start(f32[256,1024]{1,0:T(8,128)} %get-tuple-element.6) | copy-start | bytes 3145732
  341.4 5.2 slice-start.1
  352.3 91.2 %copy-start.3 = (f32[16,13312]{1,0:T(8,128)S(1)}, f32[16,13312]{1,0:T(8,128)}, u32[]{:S(2)}) copy-start(f32[16,13312]{1,0:T(8,128)} %reduce-scatter.3.cloned.1.call-done) | copy-start | bytes 2555908
  352.3 143.7 %all-gather.5.cloned.1.call-start = ((), (), s32[]{:S(2)}) async-start(), calls=%async_computation.7 | async-start | bytes 3620864 | tf_op jit(solution)/shard_map/all_gather | solution.py:25
  496.1 5.6 %copy-start.7 = (bf16[256,6656]{1,0:T(8,128)(2,1)S(1)}, bf16[256,6656]{1,0:T(8,128)(2,1)}, u32[]{:S(2)}) copy-start(bf16[256,6656]{1,0:T(8,128)(2,1)} %all-gather.5.cloned.1.call-done) | copy-start | bytes 10223620
  507.5 20.6 %all-to-all-start.1 = ((f32[8,32,1024]{2,1,0:T(8,128)}), f32[8,32,1024]{2,1,0:T(8,128)S(1)}, u32[]{:S(2)}, u32[]{:S(2)}) async-start(f32[8,32,1024]{2,1,0:T(8,128)} %bitcast.23), calls=%async_computation.3 | async-start | bytes 2097152 | tf_op jit(solution)/shard_map/all_to_all | solution.py:39
Sparse Core Ops, SparseCore 0:
  42.6 128.4 reduce-scatter.2
  173.6 49.7 all-gather.2
  236.1 103.6 all-reduce.2
  352.5 91.0 reduce-scatter.4
  445.9 50.1 all-gather.4
where the time goes:
time: 536 us; the launch traced here: 535 us
  waiting for transfers between devices  439 us (82%)
  matrix products  51.5 us (10%)
  other arithmetic  15.1 us (3%)
  between operations  13.4 us (2%)
  starting transfers between devices  11.2 us (2%)
  local copies, waits for them, and re-layouts  5.77 us (1%)
    reduce_scatter x1, waiting for transfers between devices, on_device(): lax.psum_scatter(jnp.concatenate(project_in(gathered, probe, gate_weight,...  129 us
    psum x1, waiting for transfers between devices, on_device(): output, out_tan = lax.psum((out_pieces[0], out_pieces[1]), 'row')  102 us
    all_gather x2, waiting for transfers between devices, side_by_side(): lax.all_gather(both, axis, axis=dim, tiled=True)  101 us
    reduce_scatter x1, waiting for transfers between devices, on_device(): lax.psum_scatter(jnp.concatenate(paired(cotangent, cot_half, down_weight,...  91.2 us
    dot_general x6, matrix products, matmul(): return jnp.dot(left_rows, weight, preferred_element_type=jnp.float32)  32.8 us
    dot_general x4, matrix products, matmul_trans(): lax.dot_general(left_rows, weight, (((1,), (1,)), ((), ())), preferred_el...  18.7 us
    all_to_all x1, waiting for transfers between devices, summed_on_arrival(): lax.all_to_all(pieces, axis, split_axis=0, concat_axis=0, tiled=True)  16.2 us
  transfers between devices with their start and end apart: 7, of which 6 were waited for; matrix products, arithmetic and copies ran while one was open for 3% of the time, Pallas kernels for 0%

commit v1 on v0

v1 whole, which is shorter than its diff:
```python
import functools
import math

import jax
import jax.numpy as jnp
from jax import lax
from jax.experimental import pallas as pl
from jax.experimental.pallas import tpu as pltpu
from jax.sharding import PartitionSpec as P

MESH = pl.DeviceIdType.MESH
F32, BF16, I16, I32 = jnp.float32, jnp.bfloat16, jnp.int16, jnp.int32

TOK = 256
KD = 1024
HW = 3328
CW = 256
NJ = HW // CW
NF = KD // CW
LAG = (0, 2, 5, 8, 11, 14, 17, 20, 22)
SLOTS = 10

CODE_UNIT = 1024.0
CODE_SCALE = 32700.0 / math.log1p(4700.0 * CODE_UNIT)


def log_encode(x):
    mag = jnp.log(1.0 + jnp.abs(x) * CODE_UNIT) * CODE_SCALE
    q = (mag + 0.5).astype(I32)
    return jnp.where(x < 0, -q, q).astype(I16)


def log_decode(y):
    y = y.astype(I32).astype(F32)
    mag = (jnp.exp(jnp.abs(y) * (1.0 / CODE_SCALE)) - 1.0) * (1.0 / CODE_UNIT)
    return jnp.where(y < 0, -mag, mag)


def bf_encode(x):
    return x.astype(BF16)


def bf_decode(x):
    return x.astype(F32)


def dot(a, b):
    return jnp.dot(a, b, preferred_element_type=F32)


def dot_t(a, b):
    return lax.dot_general(a, b, (((1,), (1,)), ((), ())), preferred_element_type=F32)


def silu_parts(pre_act):
    sig = 1.0 / (1.0 + jnp.exp(-pre_act))
    active = pre_act * sig
    slopes = sig * (1.0 + pre_act * (1.0 - sig))
    curves = sig * (1.0 - sig) * (2.0 + pre_act * (1.0 - 2.0 * sig))
    return active, slopes, curves


def rdma(src, dst, ssem, rsem, dev):
    return pltpu.make_async_remote_copy(
        src_ref=src, dst_ref=dst, send_sem=ssem, recv_sem=rsem, device_id=dev, device_id_type=MESH
    )


class Ring:
    def __init__(self, pos, plus, minus, mate, side, rows, code, bufs, sems, x_code):
        self.pos, self.plus, self.minus, self.mate, self.side = pos, plus, minus, mate, side
        self.rows, self.half = rows, rows // 2
        self.enc, self.dec = code
        self.x_enc, self.x_dec = x_code
        self.opp_s, self.opp_r, self.nb_s, self.nb_r, self.x_s, self.x_r, self.keep = bufs
        self.ss, self.rs = sems

    def block(self, delta):
        return pl.multiple_of(lax.rem(self.pos + (4 + delta), 4) * self.rows, self.rows)

    def opp_copy(self, k, p):
        dev = self.plus if p == 0 else self.minus
        sl = lax.rem(k, SLOTS)
        return rdma(self.opp_s.at[sl, p], self.opp_r.at[k, p], self.ss.at[k, p], self.rs.at[k, p], dev)

    def nb_copy(self, k, d):
        dev = self.plus if d == 0 else self.minus
        sl = lax.rem(k, SLOTS)
        return rdma(self.nb_s.at[sl, d], self.nb_r.at[k, d], self.ss.at[k, 2 + d], self.rs.at[k, 2 + d], dev)

    def x_copy(self, k):
        sl = lax.rem(k, SLOTS)
        return rdma(self.x_s.at[sl], self.x_r.at[k], self.ss.at[k, 4], self.rs.at[k, 4], self.mate)

    def scatter(self, k, term):
        sl = lax.rem(k, SLOTS)
        for p in range(2):
            self.opp_s[sl, p] = self.enc(term(self.block(2), p))
        for p in range(2):
            self.opp_copy(k, p).start()
        self.keep[sl, 0] = term(self.block(1), 0)
        self.nb_s[sl, 0, 1] = self.enc(term(self.block(1), 1))
        self.nb_s[sl, 1, 0] = self.enc(term(self.block(-1), 0))
        self.keep[sl, 1] = term(self.block(-1), 1)
        for p in range(2):
            self.keep[sl, 2 + p] = term(self.block(0), p)

    def relay(self, k):
        sl = lax.rem(k, SLOTS)
        for p in range(2):
            self.opp_copy(k, p).wait()
            self.nb_s[sl, p, p] = self.enc(self.keep[sl, p] + self.dec(self.opp_r[k, p]))
            self.nb_copy(k, p).start()

    def gather_in(self, k):
        sl = lax.rem(k, SLOTS)
        for d in range(2):
            self.nb_copy(k, d).wait()
        other = pl.multiple_of((1 - self.side) * self.half, self.half)
        for p in range(2):
            self.keep[sl, 2 + p] += self.dec(self.nb_r[k, 0, p]) + self.dec(self.nb_r[k, 1, p])
            self.x_s[sl, p] = self.x_enc(self.keep[sl, 2 + p, pl.ds(other, self.half), :])
        self.x_copy(k).start()

    def finish(self, k):
        sl = lax.rem(k, SLOTS)
        self.x_copy(k).wait()
        own = pl.multiple_of(self.side * self.half, self.half)
        return [
            self.keep[sl, 2 + p, pl.ds(own, self.half), :] + self.x_dec(self.x_r[k, p]) for p in range(2)
        ]


class Spread:
    def __init__(self, pos, plus, minus, mate, side, rows, base, region, sems):
        self.pos, self.plus, self.minus, self.mate, self.side = pos, plus, minus, mate, side
        self.rows, self.half, self.base, self.region = rows, rows // 2, base, region
        self.ss, self.rs = sems

    def start_of(self, delta):
        return pl.multiple_of(self.base + lax.rem(self.pos + (4 + delta), 4) * self.rows, self.rows)

    def copy(self, k, i, ref, dev):
        return rdma(ref, ref, self.ss.at[k, i], self.rs.at[k, i], dev)

    def mine(self, k):
        at = pl.multiple_of(self.start_of(0) + self.side * self.half, self.half)
        return self.copy(k, 0, self.region(k, at, self.half, None), self.mate)

    def first(self, k):
        self.mine(k).start()

    def second(self, k):
        self.mine(k).wait_send()
        at = pl.multiple_of(self.start_of(0) + (1 - self.side) * self.half, self.half)
        self.copy(k, 0, self.region(k, at, self.half, None), self.mate).wait_recv()
        ref = self.region(k, self.start_of(0), self.rows, None)
        self.copy(k, 1, ref, self.plus).start()
        self.copy(k, 2, ref, self.minus).start()

    def third(self, k):
        ref = self.region(k, self.start_of(0), self.rows, None)
        self.copy(k, 1, ref, self.plus).wait_send()
        self.copy(k, 2, ref, self.minus).wait_send()
        self.copy(k, 1, self.region(k, self.start_of(-1), self.rows, None), self.plus).wait_recv()
        self.copy(k, 3, self.region(k, self.start_of(-1), self.rows, 0), self.plus).start()
        self.copy(k, 2, self.region(k, self.start_of(1), self.rows, None), self.minus).wait_recv()
        self.copy(k, 4, self.region(k, self.start_of(1), self.rows, 1), self.minus).start()

    def last(self, k):
        self.copy(k, 3, self.region(k, self.start_of(-1), self.rows, 0), self.plus).wait_send()
        self.copy(k, 4, self.region(k, self.start_of(1), self.rows, 1), self.minus).wait_send()
        self.copy(k, 3, self.region(k, self.start_of(2), self.rows, 0), self.plus).wait_recv()
        self.copy(k, 4, self.region(k, self.start_of(2), self.rows, 1), self.minus).wait_recv()


def block_kernel(
    tok_ref,
    words_ref,
    wt_ref,
    gate_hbm,
    up_hbm,
    down_hbm,
    out_ref,
    wg,
    wu,
    wd,
    lhs,
    cot,
    hid,
    back,
    res,
    d2d,
    keep,
    opp_s,
    opp_r,
    nb_s,
    nb_r,
    x_s,
    x_r,
    opp_sb,
    opp_rb,
    nb_sb,
    nb_rb,
    x_sb,
    x_rb,
    pre,
    rkeep,
    ropp_s,
    ropp_r,
    rnb_s,
    rnb_r,
    rx_s,
    rx_r,
    rres,
    own_tan,
    w_sem,
    d_send,
    d_recv,
    c_send,
    c_recv,
    cb_send,
    cb_recv,
    g_send,
    g_recv,
    gb_send,
    gb_recv,
    r_send,
    r_recv,
    s_send,
    s_recv,
):
    r, c = lax.axis_index("row"), lax.axis_index("col")
    z, x_lo = r // 2, r % 2
    y, x_hi, core = c // 4, (c // 2) % 2, c % 2
    core_mate = (r, c + 1 - 2 * core)
    x_mate = (r, c + 2 - 4 * x_hi)
    y_plus, y_minus = (r, lax.rem(c + 4, 16)), (r, lax.rem(c + 12, 16))
    z_plus, z_minus = (lax.rem(r + 2, 8), c), (lax.rem(r + 6, 8), c)
    lo_mate = (r + 1 - 2 * x_lo, c)

    def weight_copy(j, which):
        cols = pl.ds(pl.multiple_of(j * CW, CW), CW)
        src, dst = (gate_hbm, wg) if which == 0 else (up_hbm, wu)
        return pltpu.make_async_copy(src.at[:, cols], dst.at[:, cols], w_sem.at[which, j])

    def down_copy():
        return pltpu.make_async_copy(down_hbm, wd, w_sem.at[0, NJ])

    def start_weights(j, _):
        weight_copy(j, 0).start()
        weight_copy(j, 1).start()
        return 0

    lax.fori_loop(0, NJ, start_weights, 0)

    barrier = pltpu.get_barrier_semaphore()
    mates = (core_mate, x_mate, y_plus, y_minus, z_plus, z_minus, lo_mate)
    for dev in mates:
        pl.semaphore_signal(barrier, inc=1, device_id=dev, device_id_type=MESH)

    own_rows = pl.multiple_of(r * 32, 32)
    lhs[1, pl.ds(own_rows, 32), :] = tok_ref[...]
    pl.semaphore_wait(barrier, len(mates))

    def tok_region(k, at, rows, half):
        if half is None:
            return lhs.at[1, pl.ds(at, rows), :]
        return lhs.at[1, pl.ds(at, rows), pl.ds(half * (KD // 2), KD // 2)]

    def cot_region(k, at, rows, half):
        cols = pl.ds(pl.multiple_of(k * CW, CW), CW)
        if half is None:
            return cot.at[:, pl.ds(at, rows), cols]
        return cot.at[pl.ds(half, 1), pl.ds(at, rows), cols]

    def wide_region(ref):
        def region(k, at, rows, half):
            cols = pl.ds(pl.multiple_of(k * CW, CW), CW)
            if half is None:
                return ref.at[:, pl.ds(at, rows), cols]
            return ref.at[pl.ds(half, 1), pl.ds(at, rows), cols]

        return region

    tok_spread = Spread(z, z_plus, z_minus, lo_mate, x_lo, 64, 0, tok_region, (s_send, s_recv))
    cot_spread = Spread(z, z_plus, z_minus, lo_mate, x_lo, 64, 0, cot_region, (s_send, s_recv))
    hid_spread = Spread(y, y_plus, y_minus, x_mate, x_hi, 32, core * 128, wide_region(hid), (g_send, g_recv))
    back_spread = Spread(y, y_plus, y_minus, x_mate, x_hi, 32, core * 128, wide_region(back), (gb_send, gb_recv))
    pre_ring = Ring(
        y, y_plus, y_minus, x_mate, x_hi, 32, (log_encode, log_decode),
        (opp_s, opp_r, nb_s, nb_r, x_s, x_r, keep), (c_send, c_recv), (log_encode, log_decode),
    )
    back_ring = Ring(
        y, y_plus, y_minus, x_mate, x_hi, 32, (bf_encode, bf_decode),
        (opp_sb, opp_rb, nb_sb, nb_rb, x_sb, x_rb, keep), (cb_send, cb_recv), (bf_encode, bf_decode),
    )
    row_ring = Ring(
        z, z_plus, z_minus, lo_mate, x_lo, 64, (bf_encode, bf_decode),
        (ropp_s, ropp_r, rnb_s, rnb_r, rx_s, rx_r, rkeep), (r_send, r_recv), (lambda v: v, lambda v: v),
    )

    tok_spread.first(NF)

    words = words_ref[...]
    parts = [lax.shift_right_logical(words, jnp.full_like(words, 8 * b)) & 255 for b in range(4)]
    octets = jnp.concatenate(parts, axis=0).astype(F32).astype(BF16)
    at = lax.broadcasted_iota(I32, (128, KD), 0)
    lane = lax.broadcasted_iota(I32, (128, KD), 1)
    pick = ((at % 32) * 4 + at // 32 == lane // 8).astype(F32).astype(BF16)
    spread = lax.dot_general(octets, pick, (((0,), (0,)), ((), ())), preferred_element_type=F32)
    bit = lax.broadcasted_iota(I32, (TOK, KD), 1) % 8
    signs = 2 * (lax.shift_right_logical(spread.astype(I32), bit) & 1) - 1
    lhs[0] = signs.astype(F32).astype(BF16)

    core_rows = pl.multiple_of(core * 128, 128)
    mate_rows = pl.multiple_of((1 - core) * 128, 128)
    share_rows = pl.multiple_of(core * 128 + y * 32 + x_hi * 16, 16)

    def core_copy(kk):
        sl = lax.rem(kk, 4)
        return rdma(
            res.at[sl, :, pl.ds(mate_rows, 128), :], d2d.at[kk], d_send.at[kk], d_recv.at[kk], core_mate
        )

    def wide_copy(ref, k, rows, sems):
        cols = pl.ds(pl.multiple_of(k * CW, CW), CW)
        part = ref.at[:, pl.ds(rows, 128), cols]
        return rdma(part, part, sems[0].at[k, 5], sems[1].at[k, 5], core_mate)

    def chip_term(kk):
        sl = lax.rem(kk, 4)

        def term(block, p):
            rows = pl.multiple_of(core_rows + block, 32)
            return res[sl, p, pl.ds(rows, 32), :] + d2d[kk, p, pl.ds(block, 32), :]

        return term

    def stage(t, lag, low, high, work):
        k = t - lag

        @pl.when((k >= low) & (k < high))
        def _():
            work(k)

    def sweep(count, first_gather, base, multiply, ring, spreader, wide, sems, shares, extra):
        def begin(k):
            multiply(k)
            core_copy(base + k).start()

        def chip_sum(k):
            core_copy(base + k).wait()
            ring.scatter(k, chip_term(base + k))

        def shared(k):
            shares(k, ring.finish(k))

        def to_mate(j):
            spreader.last(j)
            wide_copy(wide, j, core_rows, sems).start()

        def from_mate(j):
            wide_copy(wide, j, core_rows, sems).wait_send()
            wide_copy(wide, j, mate_rows, sems).wait_recv()

        def step(t, _):
            gt = t - first_gather
            stage(gt, LAG[8], 0, NJ, from_mate)
            stage(gt, LAG[7], 0, NJ, to_mate)
            stage(gt, LAG[6], 0, NJ, spreader.third)
            stage(gt, LAG[5], 0, NJ, spreader.second)
            stage(t, LAG[4], 0, count, shared)
            stage(gt, LAG[4], 0, NJ, spreader.first)
            stage(t, LAG[3], 0, count, ring.gather_in)
            stage(t, LAG[2], 0, count, ring.relay)
            stage(t, LAG[1], 0, count, chip_sum)
            if extra is not None:
                extra(t)
            stage(t, LAG[0], 0, count, begin)
            return 0

        lax.fori_loop(0, count + LAG[8], step, 0)

    def cols_of(k):
        return pl.ds(pl.multiple_of(k * CW, CW), CW)

    def multiply_in(k):
        j, which = k % NJ, k // NJ

        @pl.when(k < NJ)
        def _():
            weight_copy(j, 0).wait()
            weight_copy(j, 1).wait()

        sl = lax.rem(k, 4)
        res[sl, 0] = dot(lhs[which], wg[:, cols_of(j)])
        res[sl, 1] = dot(lhs[which], wu[:, cols_of(j)])

    def shares_in(k, sums):
        pre[k, 0] = sums[0]
        pre[k, 1] = sums[1]

        @pl.when(k >= NJ)
        def _():
            j = k - NJ
            active, slopes, _ = silu_parts(pre[k, 0])
            up_pre, gate_tan, up_tan = pre[k, 1], pre[j, 0], pre[j, 1]
            hid[0, pl.ds(share_rows, 16), cols_of(j)] = (active * up_pre).astype(BF16)
            hid[1, pl.ds(share_rows, 16), cols_of(j)] = (
                slopes * gate_tan * up_pre + active * up_tan
            ).astype(BF16)

    def token_steps(t):
        @pl.when(t == 2)
        def _():
            tok_spread.second(NF)

        @pl.when(t == 6)
        def _():
            tok_spread.third(NF)

        @pl.when(t == 9)
        def _():
            down_copy().start()

        @pl.when(t == 11)
        def _():
            tok_spread.last(NF)

    sweep(
        2 * NJ, NJ, 0, multiply_in, pre_ring, hid_spread, hid, (g_send, g_recv), shares_in, token_steps
    )
    down_copy().wait()

    def row_term(sl):
        def term(block, p):
            return rres[sl, p, pl.ds(block, 64), :]

        return term

    def multiply_out(n):
        for q in range(2):
            rres[0, q] = dot(hid[q], wd[:, cols_of(n)])
        row_ring.scatter(n, row_term(0))

    def cotangents(n):
        out, out_tan = row_ring.finish(n)
        scale = wt_ref[pl.ds(own_rows, 32), :]
        rows, cols = pl.ds(own_rows, 32), cols_of(n)
        tan = scale * (lhs[0, rows, cols].astype(F32) + out_tan)
        own_tan[:, cols] = tan
        cot[0, rows, cols] = (scale * (lhs[1, rows, cols].astype(F32) + out)).astype(BF16)
        cot[1, rows, cols] = tan.astype(BF16)
        cot_spread.first(n)

    def out_step(t, _):
        stage(t, 6, 0, NF, cot_spread.last)
        stage(t, 5, 0, NF, cot_spread.third)
        stage(t, 4, 0, NF, cot_spread.second)
        stage(t, 3, 0, NF, cotangents)
        stage(t, 2, 0, NF, row_ring.gather_in)
        stage(t, 1, 0, NF, row_ring.relay)
        stage(t, 0, 0, NF, multiply_out)
        return 0

    lax.fori_loop(0, NF + 6, out_step, 0)

    def multiply_back(k):
        sl = lax.rem(2 * NJ + k, 4)
        rows = pl.ds(pl.multiple_of(k * CW, CW), CW)
        for q in range(2):
            res[sl, q] = dot_t(cot[q], wd[rows, :])

    def shares_back(j, sums):
        backward, back_tan = sums
        active, slopes, curves = silu_parts(pre[NJ + j, 0])
        up_pre, gate_tan, up_tan = pre[NJ + j, 1], pre[j, 0], pre[j, 1]
        gate_back = (
            back_tan * up_pre * slopes + backward * up_tan * slopes + backward * up_pre * curves * gate_tan
        )
        up_back = back_tan * active + backward * slopes * gate_tan
        back[0, pl.ds(share_rows, 16), cols_of(j)] = gate_back.astype(BF16)
        back[1, pl.ds(share_rows, 16), cols_of(j)] = up_back.astype(BF16)

    sweep(
        NJ, 0, 2 * NJ, multiply_back, back_ring, back_spread, back, (gb_send, gb_recv), shares_back, None
    )

    def multiply_last(n):
        for p in range(2):
            rows = pl.ds(pl.multiple_of((n - NF) * 2 * CW + p * CW, CW), CW)
            rres[1, p] = dot_t(back[0], wg[rows, :]) + dot_t(back[1], wu[rows, :])
        row_ring.scatter(n, row_term(1))

    def finish_last(n):
        sums = row_ring.finish(n)
        for p in range(2):
            cols = pl.ds(pl.multiple_of((n - NF) * 2 * CW + p * CW, CW), CW)
            out_ref[:, cols] = own_tan[:, cols] + sums[p]

    def last_step(t, _):
        stage(t, 3 - NF, NF, NF + 2, finish_last)
        stage(t, 2 - NF, NF, NF + 2, row_ring.gather_in)
        stage(t, 1 - NF, NF, NF + 2, row_ring.relay)
        stage(t, 0 - NF, NF, NF + 2, multiply_last)
        return 0

    lax.fori_loop(0, 2 + 3, last_step, 0)


def block(tokens, words, weight_tok, gate_weight, up_weight, down_weight):
    vmem = lambda shape, dtype: pltpu.VMEM(shape, dtype)
    sem = lambda *shape: pltpu.SemaphoreType.DMA(shape)
    anywhere = pl.BlockSpec(memory_space=pl.ANY)
    inside = pl.BlockSpec(memory_space=pltpu.VMEM)
    NC = 2 * NJ
    return pl.pallas_call(
        block_kernel,
        out_shape=jax.ShapeDtypeStruct((32, KD), F32),
        in_specs=[inside, inside, inside, anywhere, anywhere, anywhere],
        out_specs=inside,
        scratch_shapes=[
            vmem((KD, HW), BF16),
            vmem((KD, HW), BF16),
            vmem((HW, KD), BF16),
            vmem((2, TOK, KD), BF16),
            vmem((2, TOK, KD), BF16),
            vmem((2, TOK, HW), BF16),
            vmem((2, TOK, HW), BF16),
            vmem((4, 2, TOK, CW), F32),
            vmem((NC + NJ, 2, 128, CW), F32),
            vmem((SLOTS, 4, 32, CW), F32),
            vmem((SLOTS, 2, 32, CW), I16),
            vmem((NC, 2, 32, CW), I16),
            vmem((SLOTS, 2, 2, 32, CW), I16),
            vmem((NC, 2, 2, 32, CW), I16),
            vmem((SLOTS, 2, 16, CW), I16),
            vmem((NC, 2, 16, CW), I16),
            vmem((SLOTS, 2, 32, CW), BF16),
            vmem((NJ, 2, 32, CW), BF16),
            vmem((SLOTS, 2, 2, 32, CW), BF16),
            vmem((NJ, 2, 2, 32, CW), BF16),
            vmem((SLOTS, 2, 16, CW), BF16),
            vmem((NJ, 2, 16, CW), BF16),
            vmem((NC, 2, 16, CW), F32),
            vmem((SLOTS, 4, 64, CW), F32),
            vmem((SLOTS, 2, 64, CW), BF16),
            vmem((NF + 2, 2, 64, CW), BF16),
            vmem((SLOTS, 2, 2, 64, CW), BF16),
            vmem((NF + 2, 2, 2, 64, CW), BF16),
            vmem((SLOTS, 2, 32, CW), F32),
            vmem((NF + 2, 2, 32, CW), F32),
            vmem((2, 2, TOK, CW), F32),
            vmem((32, KD), F32),
            sem(2, NJ + 1),
            sem(NC + NJ),
            sem(NC + NJ),
            sem(NC, 5),
            sem(NC, 5),
            sem(NJ, 5),
            sem(NJ, 5),
            sem(NJ, 6),
            sem(NJ, 6),
            sem(NJ, 6),
            sem(NJ, 6),
            sem(NF + 2, 5),
            sem(NF + 2, 5),
            sem(NF + 1, 5),
            sem(NF + 1, 5),
        ],
        compiler_params=pltpu.CompilerParams(
            collective_id=0, has_side_effects=True, vmem_limit_bytes=67043328
        ),
    )(tokens, words, weight_tok, gate_weight, up_weight, down_weight)


def on_device(tokens, probe_words, token_ids, loss_weight, gate_weight, up_weight, down_weight):
    weight_tok = jnp.take(loss_weight, token_ids)[:, None]
    return block(tokens, probe_words.T, weight_tok, gate_weight, up_weight, down_weight)


def solution(mesh):
    return jax.shard_map(
        on_device,
        mesh=mesh,
        in_specs=(
            P("row", "col"),
            P(None, "col"),
            P(),
            P(),
            P("col", "row"),
            P("col", "row"),
            P("row", "col"),
        ),
        out_specs=P("row", "col"),
        check_vma=False,
    )
```

time: 536 us -> 176 us (0.33)
  waiting for transfers between devices: 439 us -> 0 us
  Pallas kernels: 0 us -> 170 us
  matrix products: 51.5 us -> 0 us
  other arithmetic: 15.1 us -> 1.38 us
  between operations: 13.4 us -> 0.01 us
  starting transfers between devices: 11.2 us -> 0 us
    reduce_scatter x2 -> x0, waiting for transfers between devices: 220 us -> none  [the longest x1 129 us: on_device(): lax.psum_scatter(jnp.concatenate(project_in(gathered, probe, gate_weight,...]
    pallas_call x0 -> x1, Pallas kernels: none -> 170 us  [block(): pl.pallas_call(block_kernel, out_shape=jax.ShapeDtypeStruct((32, KD), F32...]
    psum x1 -> x0, waiting for transfers between devices: 102 us -> none  [on_device(): output, out_tan = lax.psum((out_pieces[0], out_pieces[1]), 'row')]
    all_gather x2 -> x0, waiting for transfers between devices: 101 us -> none  [side_by_side(): lax.all_gather(both, axis, axis=dim, tiled=True)]
    dot_general x10 -> x0, matrix products: 51.5 us -> none  [the longest x6 32.8 us: matmul(): return jnp.dot(left_rows, weight, preferred_element_type=jnp.float32)]
    all_to_all x2 -> x0, waiting for transfers between devices: 16.2 us -> none  [the longest x1 16.2 us: summed_on_arrival(): lax.all_to_all(pieces, axis, split_axis=0, concat_axis=0, tiled=True)]
    all_to_all x2 -> x0, starting transfers between devices: 10.8 us -> none  [the longest x1 6.35 us: copy_for_each(): return lax.all_to_all(copies, axis, split_axis=0, concat_axis=0, tiled=True)]
    concatenate x4 -> x0, other arithmetic: 10.1 us -> none  [the longest x1 5.13 us: on_device(): jnp.concatenate(project_in(gathered, probe, gate_weight, up_weight), axis=1)]
  transfers between devices with their start and end apart: 7 -> 0, of which waited for: 6 -> 0; matrix products, arithmetic and copies ran while one was open for 3% -> 0% of each run, Pallas kernels for 0% -> 0%
where the time goes in v1:
time: 176 us
  Pallas kernels  170 us (97%)
  local copies, waits for them, and re-layouts  4.65 us (3%)
    pallas_call x1, Pallas kernels, block(): pl.pallas_call(block_kernel, out_shape=jax.ShapeDtypeStruct((32, KD), F32...  170 us

profile of v1, /device:TPU:0, one launch (start us, length us, event | category | flops | bytes accessed | tf_op | source)
XLA Modules:
  0.0 175.8 jit_solution(10043828736097599868)
XLA Ops:
  0.0 0.7 compare_select_fusion
  0.7 2.3 %gather_fusion = f32[256]{0:T(256)S(1)} fusion(f32[128256]{0:T(1024)} %param.10, s32[1024]{0:T(1024)S(1)} %pad_clamp_fusion), kind=kCustom, calls=%fused_computation | custom fusion | bytes 3072 | tf_op jit(solution)/shard_map/jit(_take)/gather | solution.py:579
  3.0 0.7 and_select_fusion
  3.7 0.8 copy.8.wt_ref
  4.5 169.8 %shard_map.73 = f32[32,1024]{1,0:T(8,128)} custom-call(bf16[32,1024]{1,0:T(8,128)(2,1)} %tok_ref.1, s32[32,256]{1,0:T(8,128)} %bitcast.2, f32[256,1]{1,0:T(8,128)} %copy.8.wt_ref, bf16[1024,3328]{1,0:T(8,128)(2,1)} %gate_hbm.1, bf16[1024,3328]{1,0:T(8,128)(2,1)} %up_hbm.1, bf16[3328,1024]{1,0:T(8,128)(2,1)} %down_hbm.1), custom_call_target="tpu_custom_call" | custom-call | tf_op jit(solution)/shard_map/pallas_call | solution.py:518
  174.2 1.6 copy.10
  (1 shorter events, 0.0 us)

commit v2 on v1

v2 whole, which is shorter than its diff:
```python
import functools
import math

import jax
import jax.numpy as jnp
from jax import lax
from jax.experimental import pallas as pl
from jax.experimental.pallas import tpu as pltpu
from jax.sharding import PartitionSpec as P

MESH = pl.DeviceIdType.MESH
F32, BF16, I16, I32 = jnp.float32, jnp.bfloat16, jnp.int16, jnp.int32

TOK = 256
KD = 1024
HW = 3328
CW = 256
NJ = HW // CW
NF = KD // CW
PAIRS = (NJ + 1) // 2
HP = HW + CW
LAG = (0, 1, 3, 5, 7, 9, 11, 13, 14)
NS = 4
NK = 8

CODE_UNIT = 1024.0
CODE_SCALE = 32700.0 / math.log1p(4700.0 * CODE_UNIT)


def log_encode(x):
    mag = jnp.log(1.0 + jnp.abs(x) * CODE_UNIT) * CODE_SCALE
    q = (mag + 0.5).astype(I32)
    return jnp.where(x < 0, -q, q).astype(I16)


def log_decode(y):
    y = y.astype(I32).astype(F32)
    mag = (jnp.exp(jnp.abs(y) * (1.0 / CODE_SCALE)) - 1.0) * (1.0 / CODE_UNIT)
    return jnp.where(y < 0, -mag, mag)


def bf_encode(x):
    return x.astype(BF16)


def bf_decode(x):
    return x.astype(F32)


def dot(a, b):
    return jnp.dot(a, b, preferred_element_type=F32)


def dot_t(a, b):
    return lax.dot_general(a, b, (((1,), (1,)), ((), ())), preferred_element_type=F32)


def silu_parts(pre_act):
    sig = 1.0 / (1.0 + jnp.exp(-pre_act))
    active = pre_act * sig
    slopes = sig * (1.0 + pre_act * (1.0 - sig))
    curves = sig * (1.0 - sig) * (2.0 + pre_act * (1.0 - 2.0 * sig))
    return active, slopes, curves


def rdma(src, dst, ssem, rsem, dev):
    return pltpu.make_async_remote_copy(
        src_ref=src, dst_ref=dst, send_sem=ssem, recv_sem=rsem, device_id=dev, device_id_type=MESH
    )


class Ring:
    def __init__(self, pos, plus, minus, mate, side, rows, arrays, code, bufs, sems, x_code):
        self.pos, self.plus, self.minus, self.mate, self.side = pos, plus, minus, mate, side
        self.rows, self.half = rows, rows // 2
        self.arrays, self.each = arrays, arrays // 2
        self.enc, self.dec = code
        self.x_enc, self.x_dec = x_code
        self.opp_s, self.opp_r, self.nb_s, self.nb_r, self.x_s, self.x_r, self.keep = bufs
        self.ss, self.rs = sems

    def block(self, delta):
        return pl.multiple_of(lax.rem(self.pos + (4 + delta), 4) * self.rows, self.rows)

    def opp_copy(self, k, d):
        dev = self.plus if d == 0 else self.minus
        sl, part = lax.rem(k, NS), pl.ds(d * self.each, self.each)
        return rdma(self.opp_s.at[sl, part], self.opp_r.at[sl, part], self.ss.at[sl, d], self.rs.at[sl, d], dev)

    def nb_copy(self, k, d):
        dev = self.plus if d == 0 else self.minus
        sl = lax.rem(k, NS)
        return rdma(self.nb_s.at[sl, d], self.nb_r.at[sl, d], self.ss.at[sl, 2 + d], self.rs.at[sl, 2 + d], dev)

    def x_copy(self, k):
        sl = lax.rem(k, NS)
        return rdma(self.x_s.at[sl], self.x_r.at[sl], self.ss.at[sl, 4], self.rs.at[sl, 4], self.mate)

    def scatter(self, k, term):
        sl, kp = lax.rem(k, NS), lax.rem(k, NK)
        for d in range(2):
            for i in range(d * self.each, (d + 1) * self.each):
                self.opp_s[sl, i] = self.enc(term(self.block(2), i))
            self.opp_copy(k, d).start()
        for i in range(self.arrays):
            d = i // self.each
            near, far = (1, -1) if d == 0 else (-1, 1)
            self.keep[kp, i] = term(self.block(near), i)
            self.nb_s[sl, 1 - d, i] = self.enc(term(self.block(far), i))
            self.keep[kp, self.arrays + i] = term(self.block(0), i)

    def relay(self, k):
        sl, kp = lax.rem(k, NS), lax.rem(k, NK)
        for d in range(2):
            self.opp_copy(k, d).wait()
            for i in range(d * self.each, (d + 1) * self.each):
                self.nb_s[sl, d, i] = self.enc(self.keep[kp, i] + self.dec(self.opp_r[sl, i]))
            self.nb_copy(k, d).start()

    def gather_in(self, k):
        sl, kp = lax.rem(k, NS), lax.rem(k, NK)
        for d in range(2):
            self.nb_copy(k, d).wait()
        other = pl.multiple_of((1 - self.side) * self.half, self.half)
        for i in range(self.arrays):
            own = self.arrays + i
            self.keep[kp, own] += self.dec(self.nb_r[sl, 0, i]) + self.dec(self.nb_r[sl, 1, i])
            self.x_s[sl, i] = self.x_enc(self.keep[kp, own, pl.ds(other, self.half), :])
        self.x_copy(k).start()

    def finish(self, k):
        sl, kp = lax.rem(k, NS), lax.rem(k, NK)
        self.x_copy(k).wait()
        own = pl.multiple_of(self.side * self.half, self.half)
        return [
            self.keep[kp, self.arrays + i, pl.ds(own, self.half), :] + self.x_dec(self.x_r[sl, i])
            for i in range(self.arrays)
        ]


class Spread:
    def __init__(self, pos, plus, minus, mate, side, rows, base, region, sems, slot):
        self.pos, self.plus, self.minus, self.mate, self.side = pos, plus, minus, mate, side
        self.rows, self.half, self.base, self.region = rows, rows // 2, base, region
        self.ss, self.rs = sems
        self.slot = slot

    def start_of(self, delta):
        return pl.multiple_of(self.base + lax.rem(self.pos + (4 + delta), 4) * self.rows, self.rows)

    def copy(self, k, i, ref, dev):
        sl = self.slot(k)
        return rdma(ref, ref, self.ss.at[sl, i], self.rs.at[sl, i], dev)

    def mine(self, k):
        at = pl.multiple_of(self.start_of(0) + self.side * self.half, self.half)
        return self.copy(k, 0, self.region(k, at, self.half, None), self.mate)

    def first(self, k):
        self.mine(k).start()

    def second(self, k):
        self.mine(k).wait_send()
        at = pl.multiple_of(self.start_of(0) + (1 - self.side) * self.half, self.half)
        self.copy(k, 0, self.region(k, at, self.half, None), self.mate).wait_recv()
        ref = self.region(k, self.start_of(0), self.rows, None)
        self.copy(k, 1, ref, self.plus).start()
        self.copy(k, 2, ref, self.minus).start()

    def third(self, k):
        ref = self.region(k, self.start_of(0), self.rows, None)
        self.copy(k, 1, ref, self.plus).wait_send()
        self.copy(k, 2, ref, self.minus).wait_send()
        self.copy(k, 1, self.region(k, self.start_of(-1), self.rows, None), self.plus).wait_recv()
        self.copy(k, 3, self.region(k, self.start_of(-1), self.rows, 0), self.plus).start()
        self.copy(k, 2, self.region(k, self.start_of(1), self.rows, None), self.minus).wait_recv()
        self.copy(k, 4, self.region(k, self.start_of(1), self.rows, 1), self.minus).start()

    def last(self, k):
        self.copy(k, 3, self.region(k, self.start_of(-1), self.rows, 0), self.plus).wait_send()
        self.copy(k, 4, self.region(k, self.start_of(1), self.rows, 1), self.minus).wait_send()
        self.copy(k, 3, self.region(k, self.start_of(2), self.rows, 0), self.plus).wait_recv()
        self.copy(k, 4, self.region(k, self.start_of(2), self.rows, 1), self.minus).wait_recv()


def block_kernel(
    tok_ref,
    words_ref,
    ids_ref,
    loss_hbm,
    gate_hbm,
    up_hbm,
    down_hbm,
    out_ref,
    wg,
    wu,
    wd,
    loss,
    scale,
    lhs,
    cot,
    hid,
    back,
    res,
    d2d,
    keep,
    opp_s,
    opp_r,
    nb_s,
    nb_r,
    x_s,
    x_r,
    opp_sb,
    opp_rb,
    nb_sb,
    nb_rb,
    x_sb,
    x_rb,
    pre,
    rkeep,
    ropp_s,
    ropp_r,
    rnb_s,
    rnb_r,
    rx_s,
    rx_r,
    fkeep,
    fopp_s,
    fopp_r,
    fnb_s,
    fnb_r,
    fx_s,
    fx_r,
    rres,
    own_tan,
    w_sem,
    d_send,
    d_recv,
    c_send,
    c_recv,
    g_send,
    g_recv,
    r_send,
    r_recv,
    s_send,
    s_recv,
):
    r, c = lax.axis_index("row"), lax.axis_index("col")
    z, x_lo = r // 2, r % 2
    y, x_hi, core = c // 4, (c // 2) % 2, c % 2
    core_mate = (r, c + 1 - 2 * core)
    x_mate = (r, c + 2 - 4 * x_hi)
    y_plus, y_minus = (r, lax.rem(c + 4, 16)), (r, lax.rem(c + 12, 16))
    z_plus, z_minus = (lax.rem(r + 2, 8), c), (lax.rem(r + 6, 8), c)
    lo_mate = (r + 1 - 2 * x_lo, c)

    barrier = pltpu.get_barrier_semaphore()
    mates = (core_mate, x_mate, y_plus, y_minus, z_plus, z_minus, lo_mate)
    for dev in mates:
        pl.semaphore_signal(barrier, inc=1, device_id=dev, device_id_type=MESH)

    def weight_copy(j, which):
        cols = pl.ds(pl.multiple_of(j * CW, CW), CW)
        src, dst = (gate_hbm, wg) if which == 0 else (up_hbm, wu)
        return pltpu.make_async_copy(src.at[:, cols], dst.at[:, cols], w_sem.at[which, j])

    def down_copy():
        return pltpu.make_async_copy(down_hbm, wd, w_sem.at[0, NJ])

    def loss_copy():
        return pltpu.make_async_copy(loss_hbm, loss, w_sem.at[1, NJ])

    def start_weights(j, _):
        weight_copy(j, 0).start()
        weight_copy(j, 1).start()
        return 0

    lax.fori_loop(0, NJ, start_weights, 0)
    loss_copy().start()

    own_rows = pl.multiple_of(r * 32, 32)
    lhs[1, pl.ds(own_rows, 32), :] = tok_ref[...]
    hid[:, :, :CW] = jnp.zeros((2, TOK, CW), BF16)
    back[:, :, :CW] = jnp.zeros((2, TOK, CW), BF16)

    words = words_ref[...]
    parts = [lax.shift_right_logical(words, jnp.full_like(words, 8 * b)) & 255 for b in range(4)]
    octets = jnp.concatenate(parts, axis=0).astype(F32).astype(BF16)
    at = lax.broadcasted_iota(I32, (128, KD), 0)
    lane = lax.broadcasted_iota(I32, (128, KD), 1)
    pick = ((at % 32) * 4 + at // 32 == lane // 8).astype(F32).astype(BF16)
    spread = lax.dot_general(octets, pick, (((0,), (0,)), ((), ())), preferred_element_type=F32)
    bit = lax.broadcasted_iota(I32, (TOK, KD), 1) % 8
    signs = 2 * (lax.shift_right_logical(spread.astype(I32), bit) & 1) - 1
    lhs[0] = signs.astype(F32).astype(BF16)

    pl.semaphore_wait(barrier, len(mates))

    def tok_region(k, at, rows, half):
        if half is None:
            return lhs.at[1, pl.ds(at, rows), :]
        return lhs.at[1, pl.ds(at, rows), pl.ds(half * (KD // 2), KD // 2)]

    def wide_region(ref, first, width):
        def region(k, at, rows, half):
            cols = pl.ds(pl.multiple_of((k - first) * width, width), width)
            if half is None:
                return ref.at[:, pl.ds(at, rows), cols]
            return ref.at[pl.ds(half, 1), pl.ds(at, rows), cols]

        return region

    def along_z(region, slot):
        return Spread(z, z_plus, z_minus, lo_mate, x_lo, 64, 0, region, (s_send, s_recv), slot)

    def along_y(region):
        return Spread(
            y, y_plus, y_minus, x_mate, x_hi, 32, core * 128, region, (g_send, g_recv), lambda k: lax.rem(k, NS)
        )

    tok_spread = along_z(tok_region, lambda k: NF)
    cot_spread = along_z(wide_region(cot, 0, CW), lambda k: k)
    hid_spread = along_y(wide_region(hid, 0, 2 * CW))
    back_spread = along_y(wide_region(back, PAIRS, 2 * CW))
    log_code, bf_code, plain = (log_encode, log_decode), (bf_encode, bf_decode), (lambda v: v, lambda v: v)
    y_axis, z_axis = (y, y_plus, y_minus, x_mate, x_hi), (z, z_plus, z_minus, lo_mate, x_lo)
    pre_ring = Ring(
        *y_axis, 32, 4, log_code, (opp_s, opp_r, nb_s, nb_r, x_s, x_r, keep), (c_send, c_recv), log_code
    )
    back_ring = Ring(
        *y_axis, 32, 4, bf_code, (opp_sb, opp_rb, nb_sb, nb_rb, x_sb, x_rb, keep), (c_send, c_recv), bf_code
    )
    row_ring = Ring(
        *z_axis, 64, 2, bf_code, (ropp_s, ropp_r, rnb_s, rnb_r, rx_s, rx_r, rkeep), (r_send, r_recv), plain
    )
    last_ring = Ring(
        *z_axis, 64, 2, bf_code, (fopp_s, fopp_r, fnb_s, fnb_r, fx_s, fx_r, fkeep), (r_send, r_recv), plain
    )

    tok_spread.first(NF)

    core_rows = pl.multiple_of(core * 128, 128)
    mate_rows = pl.multiple_of((1 - core) * 128, 128)
    share_rows = pl.multiple_of(core * 128 + y * 32 + x_hi * 16, 16)

    def core_copy(k):
        sl = lax.rem(k, NS)
        return rdma(res.at[sl, :, pl.ds(mate_rows, 128), :], d2d.at[sl], d_send.at[sl], d_recv.at[sl], core_mate)

    def wide_copy(spreader, k, rows):
        part = spreader.region(k, rows, 128, None)
        sl = spreader.slot(k)
        return rdma(part, part, g_send.at[sl, 5], g_recv.at[sl, 5], core_mate)

    def chip_term(k):
        sl = lax.rem(k, NS)

        def term(block, p):
            rows = pl.multiple_of(core_rows + block, 32)
            return res[sl, p, pl.ds(rows, 32), :] + d2d[sl, p, pl.ds(block, 32), :]

        return term

    def stage(t, lag, low, high, work):
        k = t - lag

        @pl.when((k >= low) & (k < high))
        def _():
            work(k)

    def sweep(low, high, shift, multiply, ring, spreader, shares, extra):
        def begin(k):
            multiply(k)
            core_copy(k).start()

        def chip_sum(k):
            core_copy(k).wait()
            ring.scatter(k, chip_term(k))

        def shared(k):
            shares(k, ring.finish(k))

        def first(k):
            spreader.first(k - shift)

        def second(k):
            spreader.second(k - shift)

        def third(k):
            spreader.third(k - shift)

        def to_mate(k):
            spreader.last(k - shift)
            wide_copy(spreader, k - shift, core_rows).start()

        def from_mate(k):
            wide_copy(spreader, k - shift, core_rows).wait_send()
            wide_copy(spreader, k - shift, mate_rows).wait_recv()

        start = high - PAIRS

        def step(t, _):
            stage(t, LAG[0], low, high, begin)
            if extra is not None:
                extra(t)
            stage(t, LAG[8], start, high, from_mate)
            stage(t, LAG[7], start, high, to_mate)
            stage(t, LAG[6], start, high, third)
            stage(t, LAG[5], start, high, second)
            stage(t, LAG[4], low, high, shared)
            stage(t, LAG[4], start, high, first)
            stage(t, LAG[3], low, high, ring.gather_in)
            stage(t, LAG[2], low, high, ring.relay)
            stage(t, LAG[1], low, high, chip_sum)
            return 0

        lax.fori_loop(low, high + LAG[8], step, 0)

    def cols_of(k):
        return pl.ds(pl.multiple_of(k * CW, CW), CW)

    def multiply_in(k):
        sl = lax.rem(k, NS)
        for u in range(2):
            n = 2 * k + u
            which, j = n // NJ, n % NJ

            @pl.when(n < NJ)
            def _():
                weight_copy(j, 0).wait()
                weight_copy(j, 1).wait()

            res[sl, 2 * u] = dot(lhs[which], wg[:, cols_of(j)])
            res[sl, 2 * u + 1] = dot(lhs[which], wu[:, cols_of(j)])

    def shares_in(k, sums):
        for u in range(2):
            n = 2 * k + u
            pre[n, 0] = sums[2 * u]
            pre[n, 1] = sums[2 * u + 1]

            @pl.when(n >= NJ)
            def _():
                j = n - NJ
                active, slopes, _ = silu_parts(pre[n, 0])
                up_pre, gate_tan, up_tan = pre[n, 1], pre[j, 0], pre[j, 1]
                hid[0, pl.ds(share_rows, 16), cols_of(j + 1)] = (active * up_pre).astype(BF16)
                hid[1, pl.ds(share_rows, 16), cols_of(j + 1)] = (
                    slopes * gate_tan * up_pre + active * up_tan
                ).astype(BF16)

    def loss_of_tokens():
        loss_copy().wait()
        lanes = lax.broadcasted_iota(I32, (1, 128), 1)

        def one(i, _):
            tid = ids_ref[own_rows + i]
            line = loss[pl.ds(tid // 128, 1), :]
            value = jnp.sum(jnp.where(lanes == tid % 128, line, 0.0), axis=1, keepdims=True)
            scale[pl.ds(i, 1), :] = jnp.broadcast_to(value, (1, 128))
            return 0

        lax.fori_loop(0, 32, one, 0)

    def token_steps(t):
        @pl.when(t == 1)
        def _():
            tok_spread.second(NF)

        @pl.when(t == 3)
        def _():
            tok_spread.third(NF)

        @pl.when(t == 5)
        def _():
            down_copy().start()
            tok_spread.last(NF)

        @pl.when(t == NJ)
        def _():
            loss_of_tokens()

    sweep(0, NJ, NJ - PAIRS, multiply_in, pre_ring, hid_spread, shares_in, token_steps)
    down_copy().wait()

    def multiply_out(n):
        for q in range(2):
            rres[q] = dot(hid[q, :, CW:], wd[:, cols_of(n)])
        row_ring.scatter(n, lambda block, p: rres[p, pl.ds(block, 64), :])

    def cotangents(n):
        out, out_tan = row_ring.finish(n)
        weight = scale[:, :1]
        rows, cols = pl.ds(own_rows, 32), cols_of(n)
        tan = weight * (lhs[0, rows, cols].astype(F32) + out_tan)
        own_tan[:, cols] = tan
        cot[0, rows, cols] = (weight * (lhs[1, rows, cols].astype(F32) + out)).astype(BF16)
        cot[1, rows, cols] = tan.astype(BF16)
        cot_spread.first(n)

    def out_step(t, _):
        stage(t, 0, 0, NF, multiply_out)
        stage(t, 12, 0, NF, cot_spread.last)
        stage(t, 10, 0, NF, cot_spread.third)
        stage(t, 8, 0, NF, cot_spread.second)
        stage(t, 6, 0, NF, cotangents)
        stage(t, 4, 0, NF, row_ring.gather_in)
        stage(t, 2, 0, NF, row_ring.relay)
        return 0

    lax.fori_loop(0, NF + 12, out_step, 0)

    def multiply_back(k):
        sl = lax.rem(k, NS)
        for u in range(2):
            j = jnp.maximum(2 * (k - NJ) - 1 + u, 0)
            rows = pl.ds(pl.multiple_of(j * CW, CW), CW)
            for q in range(2):
                res[sl, 2 * u + q] = dot_t(cot[q], wd[rows, :])

    def shares_back(k, sums):
        for u in range(2):
            j = 2 * (k - NJ) - 1 + u
            backward, back_tan = sums[2 * u], sums[2 * u + 1]

            @pl.when(j >= 0)
            def _():
                active, slopes, curves = silu_parts(pre[NJ + j, 0])
                up_pre, gate_tan, up_tan = pre[NJ + j, 1], pre[j, 0], pre[j, 1]
                gate_back = (
                    back_tan * up_pre * slopes
                    + backward * up_tan * slopes
                    + backward * up_pre * curves * gate_tan
                )
                up_back = back_tan * active + backward * slopes * gate_tan
                back[0, pl.ds(share_rows, 16), cols_of(j + 1)] = gate_back.astype(BF16)
                back[1, pl.ds(share_rows, 16), cols_of(j + 1)] = up_back.astype(BF16)

    sweep(NJ, NJ + PAIRS, NJ - PAIRS, multiply_back, back_ring, back_spread, shares_back, None)

    def multiply_last(n):
        rows = pl.ds(pl.multiple_of(n * CW, CW), CW)
        rres[0] = dot_t(back[0, :, CW:], wg[rows, :]) + dot_t(back[1, :, CW:], wu[rows, :])
        last_ring.scatter(n, lambda block, p: rres[0, pl.ds(block, 64), p * 128 : (p + 1) * 128])

    def finish_last(n):
        sums = last_ring.finish(n)
        for p in range(2):
            cols = pl.ds(pl.multiple_of(n * CW + p * 128, 128), 128)
            out_ref[:, cols] = own_tan[:, cols] + sums[p]

    def last_step(t, _):
        stage(t, 0, 0, NF, multiply_last)
        stage(t, 6, 0, NF, finish_last)
        stage(t, 4, 0, NF, last_ring.gather_in)
        stage(t, 2, 0, NF, last_ring.relay)
        return 0

    lax.fori_loop(0, NF + 6, last_step, 0)


def ring_buffers(arrays, rows, width, dtype, x_dtype):
    half = rows // 2
    shapes = ((arrays, rows), (arrays, rows), (2, arrays, rows), (2, arrays, rows))
    return [pltpu.VMEM((NS, *shape, width), dtype) for shape in shapes] + [
        pltpu.VMEM((NS, arrays, half, width), x_dtype) for _ in range(2)
    ]


def block(tokens, words, token_ids, loss_weight, gate_weight, up_weight, down_weight):
    vmem = lambda shape, dtype: pltpu.VMEM(shape, dtype)
    sem = lambda *shape: pltpu.SemaphoreType.DMA(shape)
    anywhere = pl.BlockSpec(memory_space=pl.ANY)
    inside = pl.BlockSpec(memory_space=pltpu.VMEM)
    scalars = pl.BlockSpec(memory_space=pltpu.SMEM)
    return pl.pallas_call(
        block_kernel,
        out_shape=jax.ShapeDtypeStruct((32, KD), F32),
        in_specs=[inside, inside, scalars, anywhere, anywhere, anywhere, anywhere],
        out_specs=inside,
        scratch_shapes=[
            vmem((KD, HW), BF16),
            vmem((KD, HW), BF16),
            vmem((HW, KD), BF16),
            vmem(loss_weight.shape, F32),
            vmem((32, 128), F32),
            vmem((2, TOK, KD), BF16),
            vmem((2, TOK, KD), BF16),
            vmem((2, TOK, HP), BF16),
            vmem((2, TOK, HP), BF16),
            vmem((NS, 4, TOK, CW), F32),
            vmem((NS, 4, 128, CW), F32),
            vmem((NK, 8, 32, CW), F32),
            *ring_buffers(4, 32, CW, I16, I16),
            *ring_buffers(4, 32, CW, BF16, BF16),
            vmem((2 * NJ, 2, 16, CW), F32),
            vmem((NK, 4, 64, CW), F32),
            *ring_buffers(2, 64, CW, BF16, F32),
            vmem((NK, 4, 64, 128), F32),
            *ring_buffers(2, 64, 128, BF16, F32),
            vmem((2, TOK, CW), F32),
            vmem((32, KD), F32),
            sem(2, NJ + 1),
            sem(NS),
            sem(NS),
            sem(NS, 5),
            sem(NS, 5),
            sem(NS, 6),
            sem(NS, 6),
            sem(NS, 5),
            sem(NS, 5),
            sem(NF + 1, 5),
            sem(NF + 1, 5),
        ],
        compiler_params=pltpu.CompilerParams(
            collective_id=0, has_side_effects=True, vmem_limit_bytes=67043328
        ),
    )(tokens, words, token_ids, loss_weight, gate_weight, up_weight, down_weight)


def on_device(tokens, probe_words, token_ids, loss_weight, gate_weight, up_weight, down_weight):
    return block(
        tokens, probe_words.T, token_ids, loss_weight.reshape(-1, 128), gate_weight, up_weight, down_weight
    )


def solution(mesh):
    return jax.shard_map(
        on_device,
        mesh=mesh,
        in_specs=(
            P("row", "col"),
            P(None, "col"),
            P(),
            P(),
            P("col", "row"),
            P("col", "row"),
            P("row", "col"),
        ),
        out_specs=P("row", "col"),
        check_vma=False,
    )
```

time: 176 us -> 156 us (0.89)
  Pallas kernels: 170 us -> 154 us
  local copies, waits for them, and re-layouts: 4.65 us -> 1.57 us
    pallas_call x1, Pallas kernels: 170 us -> 154 us  [block(): pl.pallas_call(block_kernel, out_shape=jax.ShapeDtypeStruct((32, KD), F32...]
    gather x1 -> x0, local copies, waits for them, and re-layouts: 2.28 us -> none  [on_device(): weight_tok = jnp.take(loss_weight, token_ids)[:, None]]
where the time goes in v2:
time: 156 us
  Pallas kernels  154 us (99%)
  local copies, waits for them, and re-layouts  1.57 us (1%)
    pallas_call x1, Pallas kernels, block(): pl.pallas_call(block_kernel, out_shape=jax.ShapeDtypeStruct((32, KD), F32...  154 us

profile of v2, /device:TPU:0, one launch (start us, length us, event | category | flops | bytes accessed | tf_op | source)
XLA Modules:
  0.0 155.7 jit_solution(13406923383391353901)
XLA Ops:
  0.0 154.1 %shard_map.73 = f32[32,1024]{1,0:T(8,128)} custom-call(bf16[32,1024]{1,0:T(8,128)(2,1)} %tok_ref.1, s32[32,256]{1,0:T(8,128)} %bitcast.3, s32[256]{0:T(256)} %ids_ref.1, f32[1002,128]{1,0:T(8,128)} %bitcast.2, bf16[1024,3328]{1,0:T(8,128)(2,1)} %gate_hbm.1, bf16[1024,3328]{1,0:T(8,128)(2,1)} %up_hbm.1, bf16[3328,1024]{1,0:T(8,128)(2,1)} %down_hbm.1), custom_call_target="tpu_custom_call" | custom-call | tf_op jit(solution)/shard_map/pallas_call | solution.py:576
  154.1 1.6 %copy.9 = f32[32,1024]{1,0:T(8,128)} copy(f32[32,1024]{1,0:T(8,128)} %shard_map.73) | data formatting | bytes 262144

commit v3 on v2

v3 whole, which is shorter than its diff:
```python
import functools
import math

import jax
import jax.numpy as jnp
from jax import lax
from jax.experimental import pallas as pl
from jax.experimental.pallas import tpu as pltpu
from jax.sharding import PartitionSpec as P

MESH = pl.DeviceIdType.MESH
F32, BF16, I16, I32 = jnp.float32, jnp.bfloat16, jnp.int16, jnp.int32

TOK = 256
HALF = 128
KD = 1024
HW = 3328
CW = 256
NJ = HW // CW
NF = KD // CW
GU = 4
NG = (2 * NJ + 2) // GU
WIN = NG * GU * CW
LAG = (0, 1, 3, 5, 7, 9, 11, 13, 14)
NS = 4
NK = 8

CODE_UNIT = 1024.0
CODE_SCALE = 32700.0 / math.log1p(4700.0 * CODE_UNIT)


def log_encode(x):
    mag = jnp.log(1.0 + jnp.abs(x) * CODE_UNIT) * CODE_SCALE
    q = (mag + 0.5).astype(I32)
    return jnp.where(x < 0, -q, q).astype(I16)


def log_decode(y):
    y = y.astype(I32).astype(F32)
    mag = (jnp.exp(jnp.abs(y) * (1.0 / CODE_SCALE)) - 1.0) * (1.0 / CODE_UNIT)
    return jnp.where(y < 0, -mag, mag)


def bf_encode(x):
    return x.astype(BF16)


def bf_decode(x):
    return x.astype(F32)


def dot(a, b):
    return jnp.dot(a, b, preferred_element_type=F32)


def dot_t(a, b):
    return lax.dot_general(a, b, (((1,), (1,)), ((), ())), preferred_element_type=F32)


def silu_parts(pre_act):
    sig = 1.0 / (1.0 + jnp.exp(-pre_act))
    active = pre_act * sig
    slopes = sig * (1.0 + pre_act * (1.0 - sig))
    curves = sig * (1.0 - sig) * (2.0 + pre_act * (1.0 - 2.0 * sig))
    return active, slopes, curves


def rdma(src, dst, ssem, rsem, dev):
    return pltpu.make_async_remote_copy(
        src_ref=src, dst_ref=dst, send_sem=ssem, recv_sem=rsem, device_id=dev, device_id_type=MESH
    )


class Ring:
    def __init__(self, pos, plus, minus, mate, side, rows, arrays, code, bufs, sems, x_code, base=0):
        self.pos, self.plus, self.minus, self.mate, self.side = pos, plus, minus, mate, side
        self.rows, self.half = rows, rows // 2
        self.arrays, self.each, self.base, self.own = arrays, arrays // 2, base, arrays + base
        self.enc, self.dec = code
        self.x_enc, self.x_dec = x_code
        self.opp_s, self.opp_r, self.nb_s, self.nb_r, self.x_s, self.x_r, self.keep = bufs
        self.ss, self.rs = sems

    def block(self, delta):
        return pl.multiple_of(lax.rem(self.pos + (4 + delta), 4) * self.rows, self.rows)

    def opp_copy(self, k, d):
        dev = self.plus if d == 0 else self.minus
        sl, part = lax.rem(k, NS), pl.ds(self.base + d * self.each, self.each)
        return rdma(self.opp_s.at[sl, part], self.opp_r.at[sl, part], self.ss.at[sl, d], self.rs.at[sl, d], dev)

    def nb_copy(self, k, d):
        dev = self.plus if d == 0 else self.minus
        sl, part = lax.rem(k, NS), pl.ds(self.base, self.arrays)
        return rdma(
            self.nb_s.at[sl, d, part], self.nb_r.at[sl, d, part], self.ss.at[sl, 2 + d], self.rs.at[sl, 2 + d], dev
        )

    def x_copy(self, k):
        sl, part = lax.rem(k, NS), pl.ds(self.base, self.arrays)
        return rdma(self.x_s.at[sl, part], self.x_r.at[sl, part], self.ss.at[sl, 4], self.rs.at[sl, 4], self.mate)

    def of(self, d):
        return range(self.base + d * self.each, self.base + (d + 1) * self.each)

    def scatter(self, k, term):
        sl, kp = lax.rem(k, NS), lax.rem(k, NK)
        for d in range(2):
            for i in self.of(d):
                self.opp_s[sl, i] = self.enc(term(self.block(2), i))
            self.opp_copy(k, d).start()
        for d in range(2):
            near, far = (1, -1) if d == 0 else (-1, 1)
            for i in self.of(d):
                self.keep[kp, i] = term(self.block(near), i)
                self.nb_s[sl, 1 - d, i] = self.enc(term(self.block(far), i))
                self.keep[kp, self.own + i] = term(self.block(0), i)

    def relay(self, k):
        sl, kp = lax.rem(k, NS), lax.rem(k, NK)
        for d in range(2):
            self.opp_copy(k, d).wait()
            for i in self.of(d):
                self.nb_s[sl, d, i] = self.enc(self.keep[kp, i] + self.dec(self.opp_r[sl, i]))
            self.nb_copy(k, d).start()

    def gather_in(self, k):
        sl, kp = lax.rem(k, NS), lax.rem(k, NK)
        for d in range(2):
            self.nb_copy(k, d).wait()
        other = pl.multiple_of((1 - self.side) * self.half, self.half)
        for i in range(self.base, self.own):
            own = self.own + i
            self.keep[kp, own] += self.dec(self.nb_r[sl, 0, i]) + self.dec(self.nb_r[sl, 1, i])
            self.x_s[sl, i] = self.x_enc(self.keep[kp, own, pl.ds(other, self.half), :])
        self.x_copy(k).start()

    def finish(self, k):
        sl, kp = lax.rem(k, NS), lax.rem(k, NK)
        self.x_copy(k).wait()
        own = pl.multiple_of(self.side * self.half, self.half)
        return [
            self.keep[kp, self.own + i, pl.ds(own, self.half), :] + self.x_dec(self.x_r[sl, i])
            for i in range(self.base, self.own)
        ]


class Spread:
    def __init__(self, pos, plus, minus, mate, side, rows, base, region, sems, slot):
        self.pos, self.plus, self.minus, self.mate, self.side = pos, plus, minus, mate, side
        self.rows, self.half, self.base, self.region = rows, rows // 2, base, region
        self.ss, self.rs = sems
        self.slot = slot

    def start_of(self, delta):
        return pl.multiple_of(self.base + lax.rem(self.pos + (4 + delta), 4) * self.rows, self.rows)

    def copy(self, k, i, ref, dev):
        sl = self.slot(k)
        return rdma(ref, ref, self.ss.at[sl, i], self.rs.at[sl, i], dev)

    def mine(self, k):
        at = pl.multiple_of(self.start_of(0) + self.side * self.half, self.half)
        return self.copy(k, 0, self.region(k, at, self.half, None), self.mate)

    def first(self, k):
        self.mine(k).start()

    def second(self, k):
        self.mine(k).wait_send()
        at = pl.multiple_of(self.start_of(0) + (1 - self.side) * self.half, self.half)
        self.copy(k, 0, self.region(k, at, self.half, None), self.mate).wait_recv()
        ref = self.region(k, self.start_of(0), self.rows, None)
        self.copy(k, 1, ref, self.plus).start()
        self.copy(k, 2, ref, self.minus).start()

    def third(self, k):
        ref = self.region(k, self.start_of(0), self.rows, None)
        self.copy(k, 1, ref, self.plus).wait_send()
        self.copy(k, 2, ref, self.minus).wait_send()
        self.copy(k, 1, self.region(k, self.start_of(-1), self.rows, None), self.plus).wait_recv()
        self.copy(k, 3, self.region(k, self.start_of(-1), self.rows, 0), self.plus).start()
        self.copy(k, 2, self.region(k, self.start_of(1), self.rows, None), self.minus).wait_recv()
        self.copy(k, 4, self.region(k, self.start_of(1), self.rows, 1), self.minus).start()

    def last(self, k):
        self.copy(k, 3, self.region(k, self.start_of(-1), self.rows, 0), self.plus).wait_send()
        self.copy(k, 4, self.region(k, self.start_of(1), self.rows, 1), self.minus).wait_send()
        self.copy(k, 3, self.region(k, self.start_of(2), self.rows, 0), self.plus).wait_recv()
        self.copy(k, 4, self.region(k, self.start_of(2), self.rows, 1), self.minus).wait_recv()


class ShortRing:
    def __init__(self, pos, plus, minus, mate, far_plus, far_minus, side, rows, arrays, bufs, sems):
        self.pos, self.mate, self.side = pos, mate, side
        self.near, self.far = (plus, minus), (far_plus, far_minus)
        self.rows, self.half = rows, rows // 2
        self.arrays, self.each = arrays, arrays // 2
        self.opp_s, self.opp_r, self.nb_s, self.nb_r, self.x_s, self.x_r, self.keep = bufs
        self.ss, self.rs = sems

    def block(self, delta):
        return pl.multiple_of(lax.rem(self.pos + (4 + delta), 4) * self.rows, self.rows)

    def side_rows(self, other):
        side = 1 - self.side if other else self.side
        return pl.ds(pl.multiple_of(side * self.half, self.half), self.half)

    def opp_copy(self, k, d):
        sl, part = k % NS, pl.ds(d * self.each, self.each)
        return rdma(
            self.opp_s.at[sl, part], self.opp_r.at[sl, part], self.ss.at[sl, d], self.rs.at[sl, d], self.near[d]
        )

    def nb_copy(self, k, d, other):
        sl, i = k % NS, 2 + 2 * d + other
        dev = self.far[d] if other else self.near[d]
        src = self.nb_s.at[sl, d, :, self.side_rows(other), :]
        return rdma(src, self.nb_r.at[sl, d, other], self.ss.at[sl, i], self.rs.at[sl, i], dev)

    def x_copy(self, k):
        sl = k % NS
        return rdma(self.x_s.at[sl], self.x_r.at[sl], self.ss.at[sl, 6], self.rs.at[sl, 6], self.mate)

    def of(self, d):
        return range(d * self.each, (d + 1) * self.each)

    def scatter(self, k, term):
        sl = k % NS
        for d in range(2):
            for i in self.of(d):
                self.opp_s[sl, i] = bf_encode(term(self.block(2), i))
            self.opp_copy(k, d).start()
        for d in range(2):
            near, far = (1, -1) if d == 0 else (-1, 1)
            for i in self.of(d):
                self.keep[sl, i] = term(self.block(near), i)
                self.nb_s[sl, 1 - d, i] = bf_encode(term(self.block(far), i))
                self.keep[sl, self.arrays + i] = term(self.block(0), i)
                self.x_s[sl, i] = bf_encode(self.keep[sl, self.arrays + i, self.side_rows(1), :])
        self.x_copy(k).start()

    def relay(self, k):
        sl = k % NS
        for d in range(2):
            self.opp_copy(k, d).wait()
            for i in self.of(d):
                self.nb_s[sl, d, i] = bf_encode(self.keep[sl, i] + bf_decode(self.opp_r[sl, i]))
            for other in (1, 0):
                self.nb_copy(k, d, other).start()

    def finish(self, k):
        sl = k % NS
        self.x_copy(k).wait()
        for d in range(2):
            for other in range(2):
                self.nb_copy(k, d, other).wait()
        sums = []
        for i in range(self.arrays):
            total = self.keep[sl, self.arrays + i, self.side_rows(0), :] + bf_decode(self.x_r[sl, i])
            for d in range(2):
                for other in range(2):
                    total = total + bf_decode(self.nb_r[sl, d, other, i])
            sums.append(total)
        return sums


class ShortSpread:
    def __init__(self, pos, plus, minus, mate, far_plus, far_minus, side, rows, region, sems):
        self.pos, self.side, self.rows, self.half, self.region = pos, side, rows, rows // 2, region
        self.near, self.far, self.mate = (plus, minus), (far_plus, far_minus), mate
        self.ss, self.rs = sems

    def start_of(self, delta):
        return pl.multiple_of(lax.rem(self.pos + (4 + delta), 4) * self.rows, self.rows)

    def part(self, k, delta, other):
        side = 1 - self.side if other else self.side
        return self.region(k, pl.multiple_of(self.start_of(delta) + side * self.half, self.half), self.half, None)

    def copy(self, k, i, ref, dev):
        return rdma(ref, ref, self.ss.at[k, i], self.rs.at[k, i], dev)

    def own_copies(self, k):
        mine = self.part(k, 0, 0)
        far = [self.copy(k, 3 + d, mine, self.far[d]) for d in range(2)]
        near = [self.copy(k, 1 + d, mine, self.near[d]) for d in range(2)]
        return far + near + [self.copy(k, 0, mine, self.mate)]

    def relay_copy(self, k, d):
        return self.copy(k, 5 + d, self.region(k, self.start_of(2 * d - 1), self.rows, d), self.near[d])

    def first(self, k):
        for one in self.own_copies(k):
            one.start()

    def third(self, k):
        for d in range(2):
            self.copy(k, 1 + d, self.part(k, 2 * d - 1, 0), self.near[d]).wait_recv()
            self.copy(k, 3 + d, self.part(k, 2 * d - 1, 1), self.far[d]).wait_recv()
            self.relay_copy(k, d).start()

    def last(self, k):
        for one in self.own_copies(k):
            one.wait_send()
        self.copy(k, 0, self.part(k, 0, 1), self.mate).wait_recv()
        for d in range(2):
            self.relay_copy(k, d).wait_send()
            self.copy(k, 5 + d, self.region(k, self.start_of(2), self.rows, d), self.near[d]).wait_recv()


def block_kernel(
    tok_ref,
    words_ref,
    ids_ref,
    loss_hbm,
    gate_hbm,
    up_hbm,
    down_hbm,
    tan_ref,
    out_ref,
    wg,
    wu,
    wd,
    loss,
    scale,
    lhs,
    cot,
    hid,
    back,
    res,
    d2d,
    keep,
    opp_s,
    opp_r,
    nb_s,
    nb_r,
    x_s,
    x_r,
    opp_sb,
    opp_rb,
    nb_sb,
    nb_rb,
    x_sb,
    x_rb,
    pre,
    rkeep,
    ropp_s,
    ropp_r,
    rnb_s,
    rnb_r,
    rx_s,
    rx_r,
    fkeep,
    fopp_s,
    fopp_r,
    fnb_s,
    fnb_r,
    fx_s,
    fx_r,
    acc,
    last,
    w_sem,
    d_send,
    d_recv,
    c_send,
    c_recv,
    g_send,
    g_recv,
    r_send,
    r_recv,
    s_send,
    s_recv,
):
    r, c = lax.axis_index("row"), lax.axis_index("col")
    z, x_lo = r // 2, r % 2
    y, x_hi, core = c // 4, (c // 2) % 2, c % 2
    core_mate = (r, c + 1 - 2 * core)
    x_mate = (r, c + 2 - 4 * x_hi)
    y_plus, y_minus = (r, lax.rem(c + 4, 16)), (r, lax.rem(c + 12, 16))
    z_plus, z_minus = (lax.rem(r + 2, 8), c), (lax.rem(r + 6, 8), c)
    lo_mate = (r + 1 - 2 * x_lo, c)
    far_plus, far_minus = ((lax.rem(r + 2, 8) + 1 - 2 * x_lo, c), (lax.rem(r + 6, 8) + 1 - 2 * x_lo, c))

    barrier = pltpu.get_barrier_semaphore()
    mates = (core_mate, x_mate, y_plus, y_minus, z_plus, z_minus, lo_mate, far_plus, far_minus)
    for dev in mates:
        pl.semaphore_signal(barrier, inc=1, device_id=dev, device_id_type=MESH)

    def weight_copy(j, which):
        cols = pl.ds(pl.multiple_of(j * CW, CW), CW)
        src, dst = (gate_hbm, wg) if which == 0 else (up_hbm, wu)
        return pltpu.make_async_copy(src.at[:, cols], dst.at[:, cols], w_sem.at[which, j])

    def down_copy():
        return pltpu.make_async_copy(down_hbm, wd, w_sem.at[0, NJ])

    def loss_copy():
        return pltpu.make_async_copy(loss_hbm, loss, w_sem.at[1, NJ])

    def start_weights(j, _):
        weight_copy(j, 0).start()
        weight_copy(j, 1).start()
        return 0

    lax.fori_loop(0, NJ, start_weights, 0)
    loss_copy().start()

    own_rows = pl.multiple_of(r * 32, 32)
    stream_rows = pl.multiple_of(r * 16, 16)
    for h in range(2):
        lhs[1, h, pl.ds(stream_rows, 16), :] = tok_ref[h * 16 : (h + 1) * 16, :]
    for ref in (hid, back):
        ref[:, :, : 2 * CW] = jnp.zeros((2, HALF, 2 * CW), BF16)

    words = words_ref[...]
    parts = [lax.shift_right_logical(words, jnp.full_like(words, 8 * b)) & 255 for b in range(4)]
    octets = jnp.concatenate(parts, axis=0).astype(F32).astype(BF16)
    at = lax.broadcasted_iota(I32, (128, KD), 0)
    lane = lax.broadcasted_iota(I32, (128, KD), 1)
    pick = ((at % 32) * 4 + at // 32 == lane // 8).astype(F32).astype(BF16)
    spread = lax.dot_general(octets, pick, (((0,), (0,)), ((), ())), preferred_element_type=F32)
    bit = lax.broadcasted_iota(I32, (TOK, KD), 1) % 8
    signs = 2 * (lax.shift_right_logical(spread.astype(I32), bit) & 1) - 1
    signs = signs.astype(F32).astype(BF16)
    for i in range(TOK // 16):
        lhs[0, i % 2, i // 2 * 16 : (i // 2 + 1) * 16, :] = signs[i * 16 : (i + 1) * 16]

    pl.semaphore_wait(barrier, len(mates))

    def tok_region(k, at, rows, half):
        if half is None:
            return lhs.at[1, :, pl.ds(at, rows), :]
        return lhs.at[1, :, pl.ds(at, rows), pl.ds(half * (KD // 2), KD // 2)]

    def wide_region(ref, shift, width):
        def region(k, at, rows, half):
            end = (k - shift + 1) * GU * CW
            cols = pl.ds(pl.multiple_of(end - width, width), width)
            if half is None:
                return ref.at[:, pl.ds(at, rows), cols]
            return ref.at[pl.ds(half, 1), pl.ds(at, rows), cols]

        return region

    def cot_region(k, at, rows, half):
        h, n = k // 2, k % 2
        cols = pl.ds(pl.multiple_of(n * 2 * CW, 2 * CW), 2 * CW)
        if half is None:
            return cot.at[h, :, pl.ds(at, rows), cols]
        return cot.at[h, pl.ds(half, 1), pl.ds(at, rows), cols]

    z_axis = (z, z_plus, z_minus, lo_mate, far_plus, far_minus, x_lo)

    def along_z(region):
        return ShortSpread(*z_axis, 32, region, (s_send, s_recv))

    def along_y(region):
        return Spread(
            y, y_plus, y_minus, x_mate, x_hi, 16, core * 64, region, (g_send, g_recv), lambda k: lax.rem(k, NS)
        )

    tok_spread = along_z(tok_region)
    cot_spread = along_z(cot_region)
    hid_spread = [along_y(wide_region(hid, 0, w * CW)) for w in (GU // 2, GU)]
    back_spread = [along_y(wide_region(back, NG, w * CW)) for w in (GU // 2, GU)]
    log_code, bf_code = (log_encode, log_decode), (bf_encode, bf_decode)
    y_axis = (y, y_plus, y_minus, x_mate, x_hi)
    pre_rings = [None, Ring(
        *y_axis, 16, 8, log_code, (opp_s, opp_r, nb_s, nb_r, x_s, x_r, keep), (c_send, c_recv), log_code
    )]
    back_bufs = (opp_sb, opp_rb, nb_sb, nb_rb, x_sb, x_rb, keep)
    back_rings = [
        Ring(*y_axis, 16, n, bf_code, back_bufs, (c_send, c_recv), bf_code, base=GU * 2 - n) for n in (GU, GU * 2)
    ]
    row_bufs = (ropp_s, ropp_r, rnb_s, rnb_r, rx_s, rx_r, rkeep)
    last_bufs = (fopp_s, fopp_r, fnb_s, fnb_r, fx_s, fx_r, fkeep)
    row_ring = ShortRing(*z_axis, 32, 4, row_bufs, (r_send, r_recv))
    last_ring = ShortRing(*z_axis, 32, 2, last_bufs, (r_send, r_recv))

    tok_spread.first(NF)

    core_rows = pl.multiple_of(core * 64, 64)
    mate_rows = pl.multiple_of((1 - core) * 64, 64)
    share_rows = pl.ds(pl.multiple_of(core * 64 + y * 16 + x_hi * 8, 8), 8)

    def core_copy(k, ring):
        sl, part = lax.rem(k, NS), pl.ds(ring.base, ring.arrays)
        return rdma(
            res.at[sl, part, pl.ds(mate_rows, 64), :], d2d.at[sl, part], d_send.at[sl], d_recv.at[sl], core_mate
        )

    def wide_copy(spreader, k, rows):
        part = spreader.region(k, rows, 64, None)
        sl = spreader.slot(k)
        return rdma(part, part, g_send.at[sl, 5], g_recv.at[sl, 5], core_mate)

    def chip_term(k):
        sl = lax.rem(k, NS)

        def term(block, p):
            rows = pl.multiple_of(core_rows + block, 16)
            return res[sl, p, pl.ds(rows, 16), :] + d2d[sl, p, pl.ds(block, 16), :]

        return term

    def stage(t, lag, low, high, work):
        k = t - lag

        @pl.when((k >= low) & (k < high))
        def _():
            work(k)

    def sweep(low, high, shift, multiply, rings, spreaders, shares, accumulate, extra, after, early=0):
        def either(first, pair, k, work):
            if pair[0] is None:
                work(pair[1])
                return
            for small, one in ((True, pair[0]), (False, pair[1])):

                @pl.when((k == first) == small)
                def _():
                    work(one)

        def ring_stage(work):
            return lambda k: either(low, rings, k, lambda ring: work(k, ring))

        def spread_stage(work):
            return lambda k: either(high - NG, spreaders, k, lambda one: work(k - shift, one))

        def start_core(k, ring):
            core_copy(k, ring).start()

        def chip_add(k, ring):
            core_copy(k, ring).wait()
            ring.scatter(k, chip_term(k))

        def send_wide(k, one):
            one.last(k)
            wide_copy(one, k, core_rows).start()

        def wait_wide(k, one):
            wide_copy(one, k, core_rows).wait_send()
            wide_copy(one, k, mate_rows).wait_recv()

        start_cores = ring_stage(start_core)

        def begin(k):
            multiply(k)
            start_cores(k)

        chip_sum = ring_stage(chip_add)
        relay = ring_stage(lambda k, ring: ring.relay(k))
        gather_in = ring_stage(lambda k, ring: ring.gather_in(k))
        shared = ring_stage(lambda k, ring: shares(k, ring.finish(k), ring.base // 2))
        first = spread_stage(lambda k, one: one.first(k))
        second = spread_stage(lambda k, one: one.second(k))
        third = spread_stage(lambda k, one: one.third(k))
        to_mate = spread_stage(send_wide)
        from_mate = spread_stage(wait_wide)

        start = high - NG

        def step(t, _):
            if early:
                stage(t, LAG[2], low, low + 1, relay)
            stage(t, LAG[0], low, high, begin)
            if extra is not None:
                extra(t)
            stage(t, LAG[8], start, high, from_mate)
            stage(t, LAG[7], start, high, to_mate)
            stage(t, LAG[6], start, high, third)
            stage(t, LAG[5], start, high, second)
            stage(t, LAG[4], low, high, shared)
            stage(t, LAG[4], start, high, first)
            stage(t, LAG[3], low, high, gather_in)
            stage(t, LAG[2], low + early, high, relay)
            stage(t, LAG[1], low, high, chip_sum)
            stage(t, LAG[8], start, high, lambda k: accumulate(k - start))
            for work in after:
                work(t)
            return 0

        lax.fori_loop(low, high + LAG[8], step, 0)

    def cols_of(k):
        return pl.ds(pl.multiple_of(k * CW, CW), CW)

    def multiply_in(k):
        sl = lax.rem(k, NS)

        def probe_chunk(u):
            j = 2 * k + u
            weight_copy(j, 0).wait()
            weight_copy(j, 1).wait()
            left = lhs[0].reshape(TOK, KD)
            for p, weight in enumerate((wg, wu)):
                both = dot(left, weight[:, cols_of(j)])
                res[sl, 4 * u + p] = both[:HALF]
                res[sl, 4 * u + 2 + p] = both[HALF:]

        def token_unit(i):
            v = GU * k + i - 2 * NJ
            for p, weight in enumerate((wg, wu)):
                res[sl, 2 * i + p] = dot(lhs[1, v // NJ], weight[:, cols_of(v % NJ)])

        @pl.when(k <= NJ // 2)
        def _():
            probe_chunk(0)

        @pl.when(k < NJ // 2)
        def _():
            probe_chunk(1)

        @pl.when(k == NJ // 2)
        def _():
            tok_spread.last(NF)

        @pl.when(k > NJ // 2)
        def _():
            token_unit(0)
            token_unit(1)

        @pl.when(k >= NJ // 2)
        def _():
            token_unit(2)
            token_unit(3)

    def shares_in(k, sums, skip):
        for i in range(GU):
            n = GU * k + i
            v = n - 2 * NJ

            @pl.when(v < 0)
            def _():
                at = n % 2 * NJ + n // 2
                pre[at, 0] = sums[2 * i]
                pre[at, 1] = sums[2 * i + 1]

            @pl.when(v >= 0)
            def _():
                pre[n, 0] = sums[2 * i]
                pre[n, 1] = sums[2 * i + 1]
                active, slopes, _ = silu_parts(pre[n, 0])
                up_pre, gate_tan, up_tan = pre[n, 1], pre[v, 0], pre[v, 1]
                hid[0, share_rows, cols_of(v + 2)] = (active * up_pre).astype(BF16)
                hid[1, share_rows, cols_of(v + 2)] = (slopes * gate_tan * up_pre + active * up_tan).astype(BF16)

    def loss_of_tokens():
        loss_copy().wait()
        lanes = lax.broadcasted_iota(I32, (1, 128), 1)

        for i in range(32):
            tid = ids_ref[own_rows + i]
            line = loss[pl.ds(tid // 128, 1), :]
            value = jnp.sum(jnp.where(lanes == tid % 128, line, 0.0), axis=1, keepdims=True)
            scale[i : i + 1, :] = jnp.broadcast_to(value, (1, 128))

    def token_spread(t):
        @pl.when(t == 3)
        def _():
            tok_spread.third(NF)

    def token_steps(t):
        @pl.when(t == 5)
        def _():
            down_copy().start()

        @pl.when(t == 8)
        def _():
            loss_of_tokens()

        @pl.when(t == NJ)
        def _():
            down_copy().wait()

    def gather_out(g):
        @pl.when(g == 0)
        def _():
            add_out(0, 2, 0, 2, True)

        @pl.when((g == 1) | (g == 2))
        def _():
            add_out(0, GU * g, GU * g - 2, GU, False)

        @pl.when(g == 3)
        def _():
            add_out(0, GU * 3, GU * 3 - 2, 3, False)
            add_out(1, GU * 3 + 3, 0, 1, True)

        @pl.when(g > 3)
        def _():
            add_out(1, GU * g, GU * g - 2 - NJ, GU, False)

    def gather_last(g):
        @pl.when(g == 3)
        def _():
            add_last(0, 1, True, pl.ds(0, KD))

        @pl.when((g > 3) & (g < NG - 1))
        def _():
            add_last(GU * g - 2 - NJ, GU, False, pl.ds(0, KD))

    def slices(first, j, units):
        width = units * CW
        return pl.ds(pl.multiple_of(first * CW, CW), width), pl.ds(pl.multiple_of(j * CW, CW), width)

    def add_out(h, first, j, units, opens):
        at, unit = slices(first, j, units)
        part = dot(hid[:, :, at].reshape(2 * HALF, units * CW), wd[unit, :])
        acc[h] = part if opens else acc[h] + part

    def add_last(j, units, opens, cols):
        part = 0.0
        for q, weight in enumerate((wg, wu)):
            at, unit = slices(j + 2, j, units)
            later, _ = slices(j + 2 + NJ, j, units)
            left = jnp.concatenate([back[q, :, at], back[q, :, later]], axis=0)
            part = part + dot_t(left, weight[cols, unit])
        last[:, cols] = part if opens else last[:, cols] + part

    def out_term(e):
        h, n = e // 2, e % 2

        def term(block, i):
            at = (2 * n + i // 2) * CW
            return acc[h, pl.ds(pl.multiple_of(i % 2 * HALF + block, 32), 32), at : at + CW]

        return term

    def cotangents(e):
        h, n = e // 2, e % 2
        sums = row_ring.finish(e)
        weight = scale[h * 16 : (h + 1) * 16, :1]
        rows = pl.ds(stream_rows, 16)
        for i in range(2):
            cols = cols_of(2 * n + i)
            tan = weight * (lhs[0, h, rows, cols].astype(F32) + sums[2 * i + 1])
            tan_ref[h * 16 : (h + 1) * 16, cols] = tan
            cot[h, 0, rows, cols] = (weight * (lhs[1, h, rows, cols].astype(F32) + sums[2 * i])).astype(BF16)
            cot[h, 1, rows, cols] = tan.astype(BF16)
        cot_spread.first(e)

    row_works = dict(
        S=lambda e: row_ring.scatter(e, out_term(e)),
        R=row_ring.relay,
        F=cotangents,
        T=cot_spread.third,
        L=cot_spread.last,
    )

    def in_order(works, names):
        for name in names.split():
            works[name[0]](int(name[1]))

    def at_steps(works, table):
        def steps(t):
            for step, names in table:

                @pl.when(t == step)
                def _():
                    in_order(works, names)

        return steps

    done = NJ - 4 + LAG[8]
    sweep(
        0, NJ, NJ - NG, multiply_in, pre_rings, hid_spread, shares_in, gather_out, token_steps,
        (token_spread, at_steps(row_works, ((done, "S0 S1"), (done + 2, "R0 R1"), (done + 3, "S2 S3")))),
    )
    in_order(row_works, "F0 F1 R2 R3 T0 T1 F2 L0 F3 L1")

    def multiply_back(k):
        @pl.when(k == NJ + 3)
        def _():
            cot_spread.last(2)
            cot_spread.last(3)

        sl = lax.rem(k, NS)
        for i in range(GU):
            v = jnp.maximum(GU * (k - NJ) - 2 + i, 0)
            left = cot[v // NJ].reshape(TOK, KD)
            both = dot_t(left, wd[pl.ds(pl.multiple_of(v % NJ * CW, CW), CW), :])
            res[sl, 2 * i] = both[:HALF]
            res[sl, 2 * i + 1] = both[HALF:]

    def shares_back(k, sums, skip):
        for i in range(skip, GU):
            v = GU * (k - NJ) - 2 + i
            backward, back_tan = sums[2 * (i - skip)], sums[2 * (i - skip) + 1]

            @pl.when(v >= 0)
            def _():
                active, slopes, curves = silu_parts(pre[2 * NJ + v, 0])
                up_pre, gate_tan, up_tan = pre[2 * NJ + v, 1], pre[v, 0], pre[v, 1]
                gate_back = (
                    back_tan * up_pre * slopes
                    + backward * up_tan * slopes
                    + backward * up_pre * curves * gate_tan
                )
                up_back = back_tan * active + backward * slopes * gate_tan
                back[0, share_rows, cols_of(v + 2)] = gate_back.astype(BF16)
                back[1, share_rows, cols_of(v + 2)] = up_back.astype(BF16)

    def last_term(f):
        h, n = f // 2, f % 2

        def term(block, i):
            at = (2 * n + i) * CW
            return last[pl.ds(pl.multiple_of(h * HALF + block, 32), 32), at : at + CW]

        return term

    def finish_last(f):
        h, n = f // 2, f % 2
        sums = last_ring.finish(f)
        for i in range(2):
            at = (2 * n + i) * CW
            out_ref[h * 16 : (h + 1) * 16, at : at + CW] = sums[i]

    last_works = dict(
        S=lambda f: last_ring.scatter(f, last_term(f)),
        R=last_ring.relay,
        F=finish_last,
    )

    sweep(
        NJ, NJ + NG, NJ - NG, multiply_back, back_rings, back_spread, shares_back, gather_last,
        None, (at_steps(row_works, ((NJ + 1, "T2"), (NJ + 2, "T3"))),), 1,
    )
    for n in range(2):
        add_last(GU * (NG - 1) - 2 - NJ, GU, False, pl.ds(n * KD // 2, KD // 2))
        in_order(last_works, f"S{n} S{n + 2}")
    in_order(last_works, "R0 R2 R1 R3 F0 F2 F1 F3")


def ring_buffers(arrays, rows, width, dtype, x_dtype):
    half = rows // 2
    shapes = ((arrays, rows), (arrays, rows), (2, arrays, rows), (2, arrays, rows))
    return [pltpu.VMEM((NS, *shape, width), dtype) for shape in shapes] + [
        pltpu.VMEM((NS, arrays, half, width), x_dtype) for _ in range(2)
    ]


def short_buffers(arrays, rows, width):
    half = rows // 2
    shapes = ((arrays, rows), (arrays, rows), (2, arrays, rows), (2, 2, arrays, half), (arrays, half), (arrays, half))
    return [pltpu.VMEM((NS, *shape, width), BF16) for shape in shapes]


def block(tokens, words, token_ids, loss_weight, gate_weight, up_weight, down_weight):
    vmem = lambda shape, dtype: pltpu.VMEM(shape, dtype)
    sem = lambda *shape: pltpu.SemaphoreType.DMA(shape)
    anywhere = pl.BlockSpec(memory_space=pl.ANY)
    inside = pl.BlockSpec(memory_space=pltpu.VMEM)
    scalars = pl.BlockSpec(memory_space=pltpu.SMEM)
    return pl.pallas_call(
        block_kernel,
        out_shape=[jax.ShapeDtypeStruct((32, KD), F32)] * 2,
        in_specs=[inside, inside, scalars, anywhere, anywhere, anywhere, anywhere],
        out_specs=[inside, inside],
        scratch_shapes=[
            vmem((KD, HW), BF16),
            vmem((KD, HW), BF16),
            vmem((HW, KD), BF16),
            vmem(loss_weight.shape, F32),
            vmem((32, 128), F32),
            vmem((2, 2, HALF, KD), BF16),
            vmem((2, 2, HALF, KD), BF16),
            vmem((2, HALF, WIN), BF16),
            vmem((2, HALF, WIN), BF16),
            vmem((NS, 8, HALF, CW), F32),
            vmem((NS, 8, HALF // 2, CW), F32),
            vmem((NK, 16, 16, CW), F32),
            *ring_buffers(8, 16, CW, I16, I16),
            *ring_buffers(8, 16, CW, BF16, BF16),
            vmem((4 * NJ, 2, 8, CW), F32),
            vmem((NS, 8, 32, CW), F32),
            *short_buffers(4, 32, CW),
            vmem((NS, 4, 32, CW), F32),
            *short_buffers(2, 32, CW),
            vmem((2, TOK, KD), F32),
            vmem((TOK, KD), F32),
            sem(2, NJ + 1),
            sem(NS),
            sem(NS),
            sem(NS, 5),
            sem(NS, 5),
            sem(NS, 6),
            sem(NS, 6),
            sem(NS, 7),
            sem(NS, 7),
            sem(NF + 1, 7),
            sem(NF + 1, 7),
        ],
        compiler_params=pltpu.CompilerParams(
            collective_id=0, has_side_effects=True, vmem_limit_bytes=67043328
        ),
    )(tokens, words, token_ids, loss_weight, gate_weight, up_weight, down_weight)


def on_device(tokens, probe_words, token_ids, loss_weight, gate_weight, up_weight, down_weight):
    tan, summed = block(
        tokens, probe_words.T, token_ids, loss_weight.reshape(-1, 128), gate_weight, up_weight, down_weight
    )
    return tan + summed


def solution(mesh):
    return jax.shard_map(
        on_device,
        mesh=mesh,
        in_specs=(
            P("row", "col"),
            P(None, "col"),
            P(),
            P(),
            P("col", "row"),
            P("col", "row"),
            P("row", "col"),
        ),
        out_specs=P("row", "col"),
        check_vma=False,
    )
```

time: 156 us -> 133 us (0.85)
  Pallas kernels: 154 us -> 131 us
  other arithmetic: 0 us -> 1.64 us
  local copies, waits for them, and re-layouts: 1.57 us -> 0 us
    pallas_call x1, Pallas kernels: 154 us -> 131 us  [block(): pl.pallas_call(block_kernel, out_shape=[jax.ShapeDtypeStruct((32, KD), F3...]
    add x0 -> x1, other arithmetic: none -> 1.64 us  [on_device(): return tan + summed]
    unnamed x1 -> x0, local copies, waits for them, and re-layouts: 1.57 us -> none
where the time goes in v3:
time: 133 us
  Pallas kernels  131 us (98%)
  other arithmetic  1.64 us (1%)
    pallas_call x1, Pallas kernels, block(): pl.pallas_call(block_kernel, out_shape=[jax.ShapeDtypeStruct((32, KD), F3...  131 us

profile of v3, /device:TPU:0, one launch (start us, length us, event | category | flops | bytes accessed | tf_op | source)
XLA Modules:
  0.0 132.8 jit_solution(12726476269975017612)
XLA Ops:
  0.0 131.2 %shard_map.73 = (f32[32,1024]{1,0:T(8,128)}, f32[32,1024]{1,0:T(8,128)}) custom-call(bf16[32,1024]{1,0:T(8,128)(2,1)} %tok_ref.1, s32[32,256]{1,0:T(8,128)} %bitcast.3, s32[256]{0:T(256)} %ids_ref.1, f32[1002,128]{1,0:T(8,128)} %bitcast.2, bf16[1024,3328]{1,0:T(8,128)(2,1)} %gate_hbm.1, bf16[1024,3328]{1,0:T(8,128)(2,1)} %up_hbm.1, bf16[3328,1024]{1,0:T(8,128)(2,1)} %down_hbm.1), custom_call_target="tpu_custom_call" | custom-call | tf_op jit(solution)/shard_map/pallas_call | solution.py:857
  131.2 1.6 %add.3 = f32[32,1024]{1,0:T(8,128)} add(f32[32,1024]{1,0:T(8,128)} %get-tuple-element.7, f32[32,1024]{1,0:T(8,128)} %get-tuple-element.8) | non-fusion elementwise | flops 32768 | bytes 393216 | tf_op jit(solution)/shard_map/add | solution.py:906

commit v4 on v3

--- a/solution.py
+++ b/solution.py
@@ -93,12 +93,17 @@
         dev = self.plus if d == 0 else self.minus
         sl, part = lax.rem(k, NS), pl.ds(self.base, self.arrays)
         return rdma(
-            self.nb_s.at[sl, d, part], self.nb_r.at[sl, d, part], self.ss.at[sl, 2 + d], self.rs.at[sl, 2 + d], dev
+            self.nb_s.at[sl, d, part], self.nb_r.at[sl, d, part], self.ss.at[sl, 2], self.rs.at[sl, 2], dev
         )
+
+    def nb_wait(self, k):
+        sl, part = lax.rem(k, NS), pl.ds(self.base, self.arrays)
+        ref = self.nb_r.at[sl, :, part]
+        rdma(ref, ref, self.ss.at[sl, 2], self.rs.at[sl, 2], self.plus).wait()
 
     def x_copy(self, k):
         sl, part = lax.rem(k, NS), pl.ds(self.base, self.arrays)
-        return rdma(self.x_s.at[sl, part], self.x_r.at[sl, part], self.ss.at[sl, 4], self.rs.at[sl, 4], self.mate)
+        return rdma(self.x_s.at[sl, part], self.x_r.at[sl, part], self.ss.at[sl, 3], self.rs.at[sl, 3], self.mate)
 
     def of(self, d):
         return range(self.base + d * self.each, self.base + (d + 1) * self.each)
@@ -126,8 +131,7 @@
 
     def gather_in(self, k):
         sl, kp = lax.rem(k, NS), lax.rem(k, NK)
-        for d in range(2):
-            self.nb_copy(k, d).wait()
+        self.nb_wait(k)
         other = pl.multiple_of((1 - self.side) * self.half, self.half)
         for i in range(self.base, self.own):
             own = self.own + i
@@ -181,13 +185,10 @@
         self.copy(k, 1, self.region(k, self.start_of(-1), self.rows, None), self.plus).wait_recv()
         self.copy(k, 3, self.region(k, self.start_of(-1), self.rows, 0), self.plus).start()
         self.copy(k, 2, self.region(k, self.start_of(1), self.rows, None), self.minus).wait_recv()
-        self.copy(k, 4, self.region(k, self.start_of(1), self.rows, 1), self.minus).start()
+        self.copy(k, 3, self.region(k, self.start_of(1), self.rows, 1), self.minus).start()
 
     def last(self, k):
-        self.copy(k, 3, self.region(k, self.start_of(-1), self.rows, 0), self.plus).wait_send()
-        self.copy(k, 4, self.region(k, self.start_of(1), self.rows, 1), self.minus).wait_send()
-        self.copy(k, 3, self.region(k, self.start_of(2), self.rows, 0), self.plus).wait_recv()
-        self.copy(k, 4, self.region(k, self.start_of(2), self.rows, 1), self.minus).wait_recv()
+        self.copy(k, 3, self.region(k, self.start_of(2), self.rows, None), self.plus).wait()
 
 
 class ShortRing:
@@ -213,14 +214,18 @@
         )
 
     def nb_copy(self, k, d, other):
-        sl, i = k % NS, 2 + 2 * d + other
+        sl = k % NS
         dev = self.far[d] if other else self.near[d]
         src = self.nb_s.at[sl, d, :, self.side_rows(other), :]
-        return rdma(src, self.nb_r.at[sl, d, other], self.ss.at[sl, i], self.rs.at[sl, i], dev)
+        return rdma(src, self.nb_r.at[sl, d, other], self.ss.at[sl, 2], self.rs.at[sl, 2], dev)
+
+    def nb_wait(self, k):
+        sl = k % NS
+        rdma(self.nb_r.at[sl], self.nb_r.at[sl], self.ss.at[sl, 2], self.rs.at[sl, 2], self.mate).wait()
 
     def x_copy(self, k):
         sl = k % NS
-        return rdma(self.x_s.at[sl], self.x_r.at[sl], self.ss.at[sl, 6], self.rs.at[sl, 6], self.mate)
+        return rdma(self.x_s.at[sl], self.x_r.at[sl], self.ss.at[sl, 3], self.rs.at[sl, 3], self.mate)
 
     def of(self, d):
         return range(d * self.each, (d + 1) * self.each)
@@ -252,9 +257,7 @@
     def finish(self, k):
         sl = k % NS
         self.x_copy(k).wait()
-        for d in range(2):
-            for other in range(2):
-                self.nb_copy(k, d, other).wait()
+        self.nb_wait(k)
         sums = []
         for i in range(self.arrays):
             total = self.keep[sl, self.arrays + i, self.side_rows(0), :] + bf_decode(self.x_r[sl, i])
@@ -279,7 +282,7 @@
         return self.region(k, pl.multiple_of(self.start_of(delta) + side * self.half, self.half), self.half, None)
 
     def copy(self, k, i, ref, dev):
-        return rdma(ref, ref, self.ss.at[k, i], self.rs.at[k, i], dev)
+        return rdma(ref, ref, self.ss.at[k, i // 5], self.rs.at[k, i], dev)
 
     def own_copies(self, k):
         mine = self.part(k, 0, 0)
@@ -288,7 +291,7 @@
         return far + near + [self.copy(k, 0, mine, self.mate)]
 
     def relay_copy(self, k, d):
-        return self.copy(k, 5 + d, self.region(k, self.start_of(2 * d - 1), self.rows, d), self.near[d])
+        return self.copy(k, 5, self.region(k, self.start_of(2 * d - 1), self.rows, d), self.near[d])
 
     def first(self, k):
         for one in self.own_copies(k):
@@ -301,12 +304,9 @@
             self.relay_copy(k, d).start()
 
     def last(self, k):
-        for one in self.own_copies(k):
-            one.wait_send()
+        self.copy(k, 0, self.region(k, 0, 5 * self.half, None), self.mate).wait_send()
         self.copy(k, 0, self.part(k, 0, 1), self.mate).wait_recv()
-        for d in range(2):
-            self.relay_copy(k, d).wait_send()
-            self.copy(k, 5 + d, self.region(k, self.start_of(2), self.rows, d), self.near[d]).wait_recv()
+        self.copy(k, 5, self.region(k, self.start_of(2), self.rows, None), self.mate).wait()
 
 
 def block_kernel(
@@ -493,7 +493,7 @@
     def wide_copy(spreader, k, rows):
         part = spreader.region(k, rows, 64, None)
         sl = spreader.slot(k)
-        return rdma(part, part, g_send.at[sl, 5], g_recv.at[sl, 5], core_mate)
+        return rdma(part, part, g_send.at[sl, 4], g_recv.at[sl, 4], core_mate)
 
     def chip_term(k):
         sl = lax.rem(k, NS)
@@ -884,14 +884,14 @@
             sem(2, NJ + 1),
             sem(NS),
             sem(NS),
+            sem(NS, 4),
+            sem(NS, 4),
             sem(NS, 5),
             sem(NS, 5),
-            sem(NS, 6),
-            sem(NS, 6),
-            sem(NS, 7),
-            sem(NS, 7),
-            sem(NF + 1, 7),
-            sem(NF + 1, 7),
+            sem(NS, 4),
+            sem(NS, 4),
+            sem(NF + 1, 2),
+            sem(NF + 1, 6),
         ],
         compiler_params=pltpu.CompilerParams(
             collective_id=0, has_side_effects=True, vmem_limit_bytes=67043328

time: 133 us -> 132 us (level)
  no operation moved by 1% of the time
where the time goes in v4:
time: 132 us
  Pallas kernels  131 us (99%)
  other arithmetic  1.64 us (1%)
    pallas_call x1, Pallas kernels, block(): pl.pallas_call(block_kernel, out_shape=[jax.ShapeDtypeStruct((32, KD), F3...  131 us

profile of v4, /device:TPU:0, one launch (start us, length us, event | category | flops | bytes accessed | tf_op | source)
XLA Modules:
  0.0 132.3 jit_solution(8532765019469738523)
XLA Ops:
  0.0 130.7 %shard_map.73 = (f32[32,1024]{1,0:T(8,128)}, f32[32,1024]{1,0:T(8,128)}) custom-call(bf16[32,1024]{1,0:T(8,128)(2,1)} %tok_ref.1, s32[32,256]{1,0:T(8,128)} %bitcast.3, s32[256]{0:T(256)} %ids_ref.1, f32[1002,128]{1,0:T(8,128)} %bitcast.2, bf16[1024,3328]{1,0:T(8,128)(2,1)} %gate_hbm.1, bf16[1024,3328]{1,0:T(8,128)(2,1)} %up_hbm.1, bf16[3328,1024]{1,0:T(8,128)(2,1)} %down_hbm.1), custom_call_target="tpu_custom_call" | custom-call | tf_op jit(solution)/shard_map/pallas_call | solution.py:857
  130.7 1.6 %add.3 = f32[32,1024]{1,0:T(8,128)} add(f32[32,1024]{1,0:T(8,128)} %get-tuple-element.7, f32[32,1024]{1,0:T(8,128)} %get-tuple-element.8) | non-fusion elementwise | flops 32768 | bytes 393216 | tf_op jit(solution)/shard_map/add | solution.py:906

commit v5 on v4

--- a/solution.py
+++ b/solution.py
@@ -317,10 +317,8 @@
     gate_hbm,
     up_hbm,
     down_hbm,
-    tan_ref,
     out_ref,
-    wg,
-    wu,
+    w_in,
     wd,
     loss,
     scale,
@@ -360,6 +358,7 @@
     fx_r,
     acc,
     last,
+    own_tan,
     w_sem,
     d_send,
     d_recv,
@@ -387,16 +386,22 @@
     for dev in mates:
         pl.semaphore_signal(barrier, inc=1, device_id=dev, device_id_type=MESH)
 
+    wg, wu = w_in.at[0], w_in.at[1]
+
+    def weight_wait(j):
+        part = w_in.at[:, :, pl.ds(pl.multiple_of(j * CW, CW), CW)]
+        pltpu.make_async_copy(part, part, w_sem.at[0, j]).wait()
+
     def weight_copy(j, which):
         cols = pl.ds(pl.multiple_of(j * CW, CW), CW)
         src, dst = (gate_hbm, wg) if which == 0 else (up_hbm, wu)
-        return pltpu.make_async_copy(src.at[:, cols], dst.at[:, cols], w_sem.at[which, j])
+        return pltpu.make_async_copy(src.at[:, cols], dst.at[:, cols], w_sem.at[0, j])
 
     def down_copy():
         return pltpu.make_async_copy(down_hbm, wd, w_sem.at[0, NJ])
 
     def loss_copy():
-        return pltpu.make_async_copy(loss_hbm, loss, w_sem.at[1, NJ])
+        return pltpu.make_async_copy(loss_hbm, loss, w_sem.at[0, NJ + 1])
 
     def start_weights(j, _):
         weight_copy(j, 0).start()
@@ -591,8 +596,7 @@
 
         def probe_chunk(u):
             j = 2 * k + u
-            weight_copy(j, 0).wait()
-            weight_copy(j, 1).wait()
+            weight_wait(j)
             left = lhs[0].reshape(TOK, KD)
             for p, weight in enumerate((wg, wu)):
                 both = dot(left, weight[:, cols_of(j)])
@@ -736,7 +740,7 @@
         for i in range(2):
             cols = cols_of(2 * n + i)
             tan = weight * (lhs[0, h, rows, cols].astype(F32) + sums[2 * i + 1])
-            tan_ref[h * 16 : (h + 1) * 16, cols] = tan
+            own_tan[h * 16 : (h + 1) * 16, cols] = tan
             cot[h, 0, rows, cols] = (weight * (lhs[1, h, rows, cols].astype(F32) + sums[2 * i])).astype(BF16)
             cot[h, 1, rows, cols] = tan.astype(BF16)
         cot_spread.first(e)
@@ -816,7 +820,8 @@
         sums = last_ring.finish(f)
         for i in range(2):
             at = (2 * n + i) * CW
-            out_ref[h * 16 : (h + 1) * 16, at : at + CW] = sums[i]
+            rows = slice(h * 16, (h + 1) * 16)
+            out_ref[rows, at : at + CW] = own_tan[rows, at : at + CW] + sums[i]
 
     last_works = dict(
         S=lambda f: last_ring.scatter(f, last_term(f)),
@@ -856,12 +861,11 @@
     scalars = pl.BlockSpec(memory_space=pltpu.SMEM)
     return pl.pallas_call(
         block_kernel,
-        out_shape=[jax.ShapeDtypeStruct((32, KD), F32)] * 2,
+        out_shape=jax.ShapeDtypeStruct((32, KD), F32),
         in_specs=[inside, inside, scalars, anywhere, anywhere, anywhere, anywhere],
-        out_specs=[inside, inside],
+        out_specs=inside,
         scratch_shapes=[
-            vmem((KD, HW), BF16),
-            vmem((KD, HW), BF16),
+            vmem((2, KD, HW), BF16),
             vmem((HW, KD), BF16),
             vmem(loss_weight.shape, F32),
             vmem((32, 128), F32),
@@ -881,7 +885,8 @@
             *short_buffers(2, 32, CW),
             vmem((2, TOK, KD), F32),
             vmem((TOK, KD), F32),
-            sem(2, NJ + 1),
+            vmem((32, KD), F32),
+            sem(1, NJ + 2),
             sem(NS),
             sem(NS),
             sem(NS, 4),
@@ -900,10 +905,9 @@
 
 
 def on_device(tokens, probe_words, token_ids, loss_weight, gate_weight, up_weight, down_weight):
-    tan, summed = block(
+    return block(
         tokens, probe_words.T, token_ids, loss_weight.reshape(-1, 128), gate_weight, up_weight, down_weight
     )
-    return tan + summed
 
 
 def solution(mesh):

time: 132 us -> 132 us (level)
  other arithmetic: 1.64 us -> 0 us
  local copies, waits for them, and re-layouts: 0 us -> 1.57 us
    add x1 -> x0, other arithmetic: 1.64 us -> none  [on_device(): return tan + summed]
    unnamed x0 -> x1, local copies, waits for them, and re-layouts: none -> 1.57 us
where the time goes in v5:
time: 132 us
  Pallas kernels  131 us (99%)
  local copies, waits for them, and re-layouts  1.57 us (1%)
    pallas_call x1, Pallas kernels, block(): pl.pallas_call(block_kernel, out_shape=jax.ShapeDtypeStruct((32, KD), F32...  131 us

profile of v5, /device:TPU:0, one launch (start us, length us, event | category | flops | bytes accessed | tf_op | source)
XLA Modules:
  0.0 132.2 jit_solution(15223974402333896495)
XLA Ops:
  0.0 130.6 %shard_map.73 = f32[32,1024]{1,0:T(8,128)} custom-call(bf16[32,1024]{1,0:T(8,128)(2,1)} %tok_ref.1, s32[32,256]{1,0:T(8,128)} %bitcast.3, s32[256]{0:T(256)} %ids_ref.1, f32[1002,128]{1,0:T(8,128)} %bitcast.2, bf16[1024,3328]{1,0:T(8,128)(2,1)} %gate_hbm.1, bf16[1024,3328]{1,0:T(8,128)(2,1)} %up_hbm.1, bf16[3328,1024]{1,0:T(8,128)(2,1)} %down_hbm.1), custom_call_target="tpu_custom_call" | custom-call | tf_op jit(solution)/shard_map/pallas_call | solution.py:862
  130.6 1.6 %copy.9 = f32[32,1024]{1,0:T(8,128)} copy(f32[32,1024]{1,0:T(8,128)} %shard_map.73) | data formatting | bytes 262144
